TPU v7x, 32 devices: a whole 2x2x4 slice. The times are simulated.
32 devices in a mesh: req: 8 (over z, x), seq: 4 (over y, core).
Axes of the slice: x: 2, y: 2, z: 4, core: 2. Of those that a mesh axis runs over, the one named last changes fastest.
Arguments:
- pool_states: float32 [104, 64, 64, 128], P('req', 'seq'), may hold values from -6 to 6
- inner_window: bfloat16 [104, 3, 4096], P('req', None, 'seq'), may hold values from -6 to 6
- state_window: bfloat16 [104, 3, 256], P('req', None, 'seq'), may hold values from -6 to 6
- move_plan: int32 [104, 2], P('req'), may hold values from 0 to 12, as said below
- active_mask: int32 [104], P('req'), may hold values 0 or 1
- inputs_inner: bfloat16 [8, 2048, 4096], P('req', 'seq'), may hold values from -6 to 6
- inputs_state: bfloat16 [8, 2048, 256], P('req', 'seq'), may hold values from -6 to 6
- gate_rows: bfloat16 [8, 2048, 4096], P('req', 'seq'), may hold values from -6 to 6
- step_raw: bfloat16 [8, 2048, 64], P('req', 'seq'), may hold values from -8 to 60
- lengths: int32 [8], P('req'), may hold values from 4 to 2048
- conv_weight: float32 [4, 4352], replicated, may hold values from -3 to 3
- conv_bias: float32 [4352], replicated, may hold values from -3 to 3
- step_bias: float32 [64], replicated, may hold values from -3.3 to -2.7
- decay_log: float32 [64], replicated, may hold values from -10 to 0
- skip_weight: float32 [64], replicated, may hold values from 0.5 to 1.5
- norm_weight: float32 [4096], replicated, may hold values from 0.25 to 1.75
Outputs:
- new_states: float32 [104, 64, 64, 128], P('req', 'seq')
- new_inner_window: bfloat16 [104, 3, 4096], P('req', None, 'seq')
- new_state_window: bfloat16 [104, 3, 256], P('req', None, 'seq')
- mixer_out: bfloat16 [8, 2048, 4096], P('req', 'seq')
Inputs may be any that keep to these rules, and one draw needn't show every extreme that they name: `move_plan`: every pair of a destination index along req and a slot 0 .. 12 is named exactly once; the rows of one device name one destination at most 4 times, and some destination exactly 4 times.
All inputs are finite; a program needn't handle non-finite values. No bound on the sum of `active_mask` on one device may be relied on, other than what follows from the above.
Results may differ from a plain program's by a relative error of at most 0.0087.
Values may be sent and summed in bfloat16 or wider, within the bound.
A program may use at most 192 MiB of HBM per device.

v0:
```python
import jax
import jax.numpy as jnp
from jax import lax
from jax.sharding import PartitionSpec as P

HEAD_DIM = 64
STATE_DIM = 128
KERNEL = 4
BLOCK_LEN = 256
PREFILLS = 1
INNER_DIM = 4096


EPSILON = 1e-05


def shifted(value, axis, steps):
    count = lax.axis_size(axis)
    leading, last = (max(0, -steps), min(count, count - steps))
    return lax.ppermute(value, axis, [(source, source + steps) for source in range(leading, last)])


def entering(shard, axis, combine, identity):
    peers, index = (lax.axis_size(axis), lax.axis_index(axis))
    everything = jax.tree.map(lambda part: lax.all_gather(part, axis), shard)
    start = jax.tree.map(
        lambda part, zero: jnp.broadcast_to(jnp.asarray(zero, part.dtype), part.shape),
        shard,
        identity,
    )

    def hop(k, before):
        reached = k < index
        new = combine(before, jax.tree.map(lambda part: part[k], everything))
        return jax.tree.map(lambda a, b: jnp.where(reached, a, b), new, before)

    return lax.fori_loop(0, peers, hop, start)


def conv_silu(window, new_rows, weight, bias_values):
    extended = jnp.concatenate([window, new_rows], axis=1).astype(jnp.float32)
    length = new_rows.shape[1]
    running = jnp.zeros(new_rows.shape, jnp.float32) + bias_values
    for offset in range(weight.shape[0]):
        running = running + weight[offset] * extended[:, offset : offset + length]
    return jax.nn.silu(running).astype(jnp.bfloat16)


def block_local(value_rows, write_rows, read_rows, step_rows, decay_rates):
    log_decay = step_rows * decay_rates
    running_log = jnp.cumsum(log_decay, axis=0)
    scores = lax.dot_general(
        read_rows, write_rows, (((1,), (1,)), ((), ())), preferred_element_type=jnp.float32
    )
    log_heads = running_log.T
    log_gaps = log_heads[:, :, None] - log_heads[:, None, :]
    positions = jnp.arange(running_log.shape[0])
    causal = positions[:, None] >= positions[None, :]
    decays = jnp.where(causal, jnp.exp(jnp.where(causal, log_gaps, 0.0)), 0.0)
    weights = (scores[None] * decays * step_rows.T[:, None, :]).astype(jnp.bfloat16)
    intra_part = jnp.einsum("hts,shp->thp", weights, value_rows, preferred_element_type=jnp.float32)
    to_end = jnp.exp(running_log[-1:] - running_log) * step_rows
    scaled = (to_end[:, :, None] * value_rows.astype(jnp.float32)).astype(jnp.bfloat16)
    block_state = jnp.einsum("shp,sn->hpn", scaled, write_rows, preferred_element_type=jnp.float32)
    return (intra_part, block_state, running_log)


def local_parts(value_rows, write_rows, read_rows, step_rows, decay_rates):
    batch_size = value_rows.shape[0]
    block_count = value_rows.shape[1] // BLOCK_LEN

    def to_items(source):
        return source.reshape((batch_size * block_count, BLOCK_LEN) + source.shape[2:])

    def from_items(source):
        return source.reshape((batch_size, block_count) + source.shape[1:])

    def one_item(pieces):
        return block_local(pieces[0], pieces[1], pieces[2], pieces[3], decay_rates)

    results = lax.map(
        one_item,
        (to_items(value_rows), to_items(write_rows), to_items(read_rows), to_items(step_rows)),
    )
    return tuple((from_items(result) for result in results))


def blocked(source):
    return source.reshape(
        (source.shape[0], source.shape[1] // BLOCK_LEN, BLOCK_LEN) + source.shape[2:]
    )


def fold_states(initial, block_states, running_logs):

    def fold_advance(carried, pieces):
        return (jnp.exp(pieces[1][:, -1])[:, :, None, None] * carried + pieces[0], None)

    final_state, unused = lax.scan(
        fold_advance, initial, (jnp.moveaxis(block_states, 1, 0), jnp.moveaxis(running_logs, 1, 0))
    )
    return final_state


def run_states(initial, block_states, running_logs, read_blocks):

    def run_advance(carried, pieces):
        block_state, running_log, read_block = pieces
        inter_part = (
            jnp.einsum(
                "bqn,bhpn->bqhp",
                read_block.astype(jnp.float32),
                carried,
                precision=lax.Precision.HIGHEST,
            )
            * jnp.exp(running_log)[:, :, :, None]
        )
        updated = jnp.exp(running_log[:, -1])[:, :, None, None] * carried + block_state
        return (updated, inter_part)

    final_state, inter_parts = lax.scan(
        run_advance,
        initial,
        (
            jnp.moveaxis(block_states, 1, 0),
            jnp.moveaxis(running_logs, 1, 0),
            jnp.moveaxis(read_blocks, 1, 0),
        ),
    )
    return (final_state, jnp.moveaxis(inter_parts, 0, 1))


def assemble(intra_part, inter_parts, value_rows, skip_own, valid_rows):
    combined = (intra_part + inter_parts).reshape(value_rows.shape) + skip_own[
        :, None
    ] * value_rows.astype(jnp.float32)
    combined = combined * valid_rows[:, :, None, None]
    return combined.astype(jnp.bfloat16).reshape(value_rows.shape[0], value_rows.shape[1], -1)


def gated_norm(payload_array, gate_part, norm_weight):
    gated_rows = payload_array.astype(jnp.float32) * jax.nn.silu(gate_part.astype(jnp.float32))
    norm_scale = lax.rsqrt(jnp.mean(gated_rows * gated_rows, axis=-1, keepdims=True) + EPSILON)
    return (gated_rows * norm_scale * norm_weight).astype(jnp.bfloat16)


def last_rows(raw_rows, positions):

    def pick_rows(source_rows, indices):
        return jnp.take(source_rows, indices, axis=0)

    return jax.vmap(pick_rows)(raw_rows, positions)


def migrate(pool_states, inner_window, state_window, move_plan, active_mask):
    slot_count = pool_states.shape[0]
    peer_count = lax.axis_size("req")
    capacity = (2 * slot_count + peer_count - 1) // peer_count
    keep_flag = active_mask.astype(jnp.float32)
    target_device = move_plan[:, 0]
    target_slot = move_plan[:, 1]
    slot_index = jnp.arange(slot_count, dtype=jnp.int32)
    earlier = (target_device[None, :] == target_device[:, None]) & (
        slot_index[None, :] < slot_index[:, None]
    )
    send_rank = jnp.sum(earlier.astype(jnp.int32), axis=1)
    matches = (target_device[None, None, :] == jnp.arange(peer_count)[:, None, None]) & (
        send_rank[None, None, :] == jnp.arange(capacity)[None, :, None]
    )
    source_slot = jnp.sum(jnp.where(matches, slot_index[None, None, :], 0), axis=2).reshape(-1)
    filled = jnp.any(matches, axis=2).reshape(-1)
    slot_tags = jnp.where(filled, jnp.take(target_slot, source_slot), -1).reshape(
        peer_count, capacity
    )

    def packed(source):
        taken_rows = jnp.take(source, source_slot, axis=0)
        return taken_rows.reshape((peer_count, capacity) + source.shape[1:])

    send_states = packed(pool_states * keep_flag[:, None, None, None])
    send_inner = packed(inner_window.astype(jnp.float32) * keep_flag[:, None, None])
    send_outer = packed(state_window.astype(jnp.float32) * keep_flag[:, None, None])
    got_states, got_inner, got_outer, got_tags = (
        lax.all_to_all(send_states, "req", split_axis=0, concat_axis=0, tiled=True),
        lax.all_to_all(send_inner, "req", split_axis=0, concat_axis=0, tiled=True),
        lax.all_to_all(send_outer, "req", split_axis=0, concat_axis=0, tiled=True),
        lax.all_to_all(slot_tags, "req", split_axis=0, concat_axis=0, tiled=True),
    )
    flat_tags = got_tags.reshape(-1)
    arrivals = jnp.arange(flat_tags.shape[0], dtype=jnp.int32)
    chosen = jnp.sum(
        jnp.where(flat_tags[None, :] == slot_index[:, None], arrivals[None, :], 0), axis=1
    )

    def placed(source):
        return jnp.take(source.reshape((-1,) + source.shape[2:]), chosen, axis=0)

    return (
        placed(got_states),
        placed(got_inner).astype(jnp.bfloat16),
        placed(got_outer).astype(jnp.bfloat16),
    )


def combine_carries(earlier_part, later_part):
    return (
        earlier_part[0] * later_part[0],
        later_part[1] + later_part[0][:, :, None, None] * earlier_part[1],
    )


def on_device(
    pool_states,
    inner_window,
    state_window,
    move_plan,
    active_mask,
    inputs_inner,
    inputs_state,
    gate_rows,
    step_raw,
    lengths,
    conv_weight,
    conv_bias,
    step_bias,
    decay_log,
    skip_weight,
    norm_weight,
):
    moved_states, moved_inner, moved_outer = migrate(
        pool_states, inner_window, state_window, move_plan, active_mask
    )
    chain_index = lax.axis_index("seq")
    chain_size = lax.axis_size("seq")
    local_length = inputs_inner.shape[1]
    local_heads = moved_states.shape[1]
    decay_rates = -jnp.exp(decay_log)
    offsets = jnp.arange(KERNEL - 1, dtype=jnp.int32)
    raw_rows = jnp.concatenate([inputs_inner, inputs_state], axis=2)
    earlier_rows = shifted(raw_rows[:, local_length - KERNEL + 1 :], "seq", 1)
    initial, head_inner, head_outer = (
        lax.all_gather(moved_states[:PREFILLS], "seq", axis=1, tiled=True),
        lax.all_gather(moved_inner[:PREFILLS].astype(jnp.float32), "seq", axis=2, tiled=True),
        lax.all_gather(moved_outer[:PREFILLS].astype(jnp.float32), "seq", axis=2, tiled=True),
    )
    first_window = jnp.concatenate([head_inner, head_outer], axis=2).astype(jnp.bfloat16)
    window = jnp.where(chain_index == 0, first_window, earlier_rows)
    mixed_rows = conv_silu(window, raw_rows, conv_weight, conv_bias)
    positions = chain_index * local_length + jnp.arange(local_length, dtype=jnp.int32)
    valid_rows = (positions[None, :] < lengths[:, None]).astype(jnp.float32)
    step_sizes = jax.nn.softplus(step_raw.astype(jnp.float32) + step_bias) * valid_rows[:, :, None]
    value_rows = mixed_rows[:, :, :INNER_DIM].reshape(PREFILLS, local_length, -1, HEAD_DIM)
    write_rows = mixed_rows[:, :, INNER_DIM : INNER_DIM + STATE_DIM]
    read_rows = mixed_rows[:, :, INNER_DIM + STATE_DIM :]
    intra_part, block_states, running_logs = local_parts(
        value_rows, write_rows, read_rows, step_sizes, decay_rates
    )
    local_end = fold_states(jnp.zeros_like(block_states[:, 0]), block_states, running_logs)
    device_decay = jnp.exp(jnp.sum(step_sizes * decay_rates, axis=1))
    every_decay = lax.all_gather(device_decay[None], "seq", axis=0, tiled=True)
    prior_decay, prior_state = entering(
        (device_decay, local_end),
        "seq",
        combine_carries,
        (jnp.ones_like(device_decay), jnp.zeros_like(local_end)),
    )
    incoming = prior_state + prior_decay[:, :, None, None] * initial
    unused_final, inter_parts = run_states(incoming, block_states, running_logs, blocked(read_rows))
    later_mask = jnp.arange(chain_size)[:, None, None] > chain_index
    suffix = jnp.prod(jnp.where(later_mask, every_decay, 1.0), axis=0)
    whole_decay = jnp.prod(every_decay, axis=0)
    window_pos = lengths[:, None] - (KERNEL - 1) + offsets[None, :] - chain_index * local_length
    inside = ((window_pos >= 0) & (window_pos < local_length)).astype(jnp.float32)
    window_term = (
        last_rows(raw_rows, jnp.clip(window_pos, 0, local_length - 1)).astype(jnp.float32)
        * inside[:, :, None]
    )
    state_sum, inner_sum, outer_sum = (
        lax.psum_scatter(
            local_end * suffix[:, :, None, None], "seq", scatter_dimension=1, tiled=True
        ),
        lax.psum_scatter(window_term[:, :, :INNER_DIM], "seq", scatter_dimension=2, tiled=True),
        lax.psum_scatter(window_term[:, :, INNER_DIM:], "seq", scatter_dimension=2, tiled=True),
    )
    own_decay = lax.dynamic_slice_in_dim(whole_decay, chain_index * local_heads, local_heads, 1)
    final_own = state_sum + own_decay[:, :, None, None] * moved_states[:PREFILLS]
    kept_inner = inner_sum.astype(jnp.bfloat16)
    kept_outer = outer_sum.astype(jnp.bfloat16)
    mixer_rows = assemble(intra_part, inter_parts, value_rows, skip_weight, valid_rows)
    mixer_out = gated_norm(mixer_rows, gate_rows, norm_weight)
    new_states = jnp.concatenate([final_own, moved_states[PREFILLS:]], axis=0)
    new_inner = jnp.concatenate([kept_inner, moved_inner[PREFILLS:]], axis=0)
    new_outer = jnp.concatenate([kept_outer, moved_outer[PREFILLS:]], axis=0)
    return (new_states, new_inner, new_outer, mixer_out)


def solution(mesh):
    return jax.shard_map(
        on_device,
        mesh=mesh,
        in_specs=(
            P("req", "seq", None, None),
            P("req", None, "seq"),
            P("req", None, "seq"),
            P("req", None),
            P("req"),
            P("req", "seq", None),
            P("req", "seq", None),
            P("req", "seq", None),
            P("req", "seq", None),
            P("req"),
            P(),
            P(),
            P(),
            P(),
            P(),
            P(),
        ),
        out_specs=(
            P("req", "seq", None, None),
            P("req", None, "seq"),
            P("req", None, "seq"),
            P("req", "seq", None),
        ),
        check_vma=False,
    )
```

profile of v0, /device:TPU:0, one launch (start us, length us, event | category | flops | bytes accessed | tf_op | source)
XLA Modules:
  0.0 568.1 jit_solution(16587530665239196977)
XLA Ops:
  10.2 7.3 %all-to-all-start = ((s32[8,1,4]{2,1,0:T(1,128)}), s32[8,1,4]{2,1,0:T(1,128)S(1)}, u32[]{:S(2)}, u32[]{:S(2)}) async-start(s32[8,1,4]{2,1,0:T(1,128)} %copy.129), calls=%async_computation | async-start | bytes 8192 | tf_op jit(solution)/shard_map/all_to_all | solution.py:187
  17.5 2.5 constant_dynamic-update-slice_fusion.1
  20.1 2.1 copy-done.7
  27.0 7.4 %broadcast_multiply_fusion = f32[13,16,64,128]{3,2,1,0:T(8,128)} fusion(f32[13,16,64,128]{3,2,1,0:T(8,128)} %param.24, f32[13]{0:T(128)S(1)} %convert_element_type.130), kind=kLoop, calls=%fused_computation.93 | loop fusion | flops 1703936 | bytes 13631540 | tf_op jit(solution)/shard_map/mul | solution.py:180
  34.3 11.2 %gather_fusion.5 = f32[32,16,64,128]{3,2,1,0:T(8,128)} fusion(f32[13,16,64,128]{3,2,1,0:T(8,128)} %broadcast_multiply_fusion, s32[1024]{0:T(1024)S(1)} %pad_clamp_fusion.1), kind=kCustom, calls=%fused_computation.5 | custom fusion | bytes 33554560 | tf_op jit(solution)/shard_map/jit(_take)/gather | solution.py:177
  46.4 12.4 %broadcast_select_fusion.2 = f32[8,4,16,64,128]{4,3,2,1,0:T(8,128)} fusion(f32[8,4,16,64,128]{4,3,2,1,0:T(8,128)} %bitcast.227, pred[8,4]{1,0:T(8,128)(4,1)S(1)} %copy.130), kind=kLoop, calls=%fused_computation.89 | loop fusion | flops 4194304 | bytes 33554464 | tf_op jit(solution)/shard_map/jit(_take)/select_n | solution.py:177
  61.4 5.8 %all-to-all-start.2 = ((bf16[8,2,384]{2,1,0:T(2,128)(2,1)}), bf16[8,2,384]{2,1,0:T(2,128)(2,1)S(1)}, u32[]{:S(2)}, u32[]{:S(2)}) async-start(bf16[8,2,384]{2,1,0:T(2,128)(2,1)} %reshape.672), calls=%async_computation.2 | async-start | bytes 24576 | tf_op jit(solution)/shard_map/all_to_all | solution.py:186
  67.2 6.5 %all-to-all-done.2 = bf16[8,2,384]{2,1,0:T(2,128)(2,1)S(1)} async-done(((bf16[8,2,384]{2,1,0:T(2,128)(2,1)}), bf16[8,2,384]{2,1,0:T(2,128)(2,1)S(1)}, u32[]{:S(2)}, u32[]{:S(2)}) %all-to-all-start.2) | async-done | bytes 12320 | tf_op jit(solution)/shard_map/all_to_all | solution.py:186
  73.7 3.4 all-to-all-start.1
  78.9 6.9 %all-reduce = f32[256]{0:T(256)S(1)} all-reduce(f32[256]{0:T(256)S(1)} %exponential_dynamic-update-slice_fusion), channel_id=2, replica_groups=mesh['req'=8,'seq'=4] {'seq'}, use_global_device_ids=true, to_apply=%add | all-reduce | flops 256 | bytes 2048
  86.2 5.8 %all-to-all-start.3 = ((f32[8,4,16,64,128]{4,3,2,1,0:T(8,128)}), f32[8,4,16,64,128]{4,3,2,1,0:T(8,128)}, u32[]{:S(2)}, u32[]{:S(2)}) async-start(f32[8,4,16,64,128]{4,3,2,1,0:T(8,128)} %broadcast_select_fusion.2), calls=%async_computation.4 | async-start | bytes 33554432 | tf_op jit(solution)/shard_map/all_to_all | solution.py:184
  94.7 5.4 all_gather.21
  101.1 5.4 all_gather.20
  106.5 3.2 maximum_convert_fusion
  109.7 5.7 %multiply_convert_fusion.5 = bf16[1,512,4352]{2,1,0:T(8,128)(2,1)S(1)} fusion(f32[1,515,4352]{2,1,0:T(8,128)S(1)} %maximum_convert_fusion, f32[4352]{0:T(1024)S(1)} %get-tuple-element.394, f32[4352]{0:T(1024)S(1)} %get-tuple-element.395, f32[4352]{0:T(1024)S(1)} %get-tuple-element.393, f32[4352]{0:T(1024)S(1)} %get-tuple-element.392, f32[4352]{0:T(1024)S(1)} %copy-done.13), kind=kLoop, calls=%fused_computation.80 | loop fusion | flops 28966912 | bytes 40195072 | tf_op jit(solution)/shard_map/convert_element_type | solution.py:46
  115.4 2.0 copy-done.6
  117.4 2.6 slice.132
  120.0 12.6 %reshape.650 = bf16[2,256,64,64]{3,2,1,0:T(8,128)(2,1)} reshape(bf16[1,512,4096]{2,1,0:T(8,128)(2,1)} %slice.132) | data formatting | bytes 8388608 | tf_op jit(solution)/shard_map/reshape;reshape | solution.py:73
  132.6 10.5 %copy.141 = bf16[2,256,64,64]{1,3,2,0:T(8,128)(2,1)} copy(bf16[2,256,64,64]{3,2,1,0:T(8,128)(2,1)} %reshape.650) | data formatting | bytes 8388608 | tf_op jit(solution)/shard_map/while | solution.py:81
  144.0 24.7 %while.53 = (s32[]{:T(128)}, f32[2,256,64,64]{1,3,2,0:T(8,128)}, f32[2,64,64,128]{3,2,1,0:T(8,128)}, f32[2,256,64]{1,2,0:T(8,128)S(1)}, bf16[2,256,64,64]{1,3,2,...) while((s32[]{:T(128)}, f32[2,256,64,64]{1,3,2,0:T(8,128)}, ...), condition=%wide.region_7.8_spmd, body=%wide.region_4.7_spmd.sunk | while | flops 852639936 | bytes 62990296 | solution.py:81
  145.4 8.0 %bitcast_dynamic-update-slice_fusion.8 = f32[2,256,64,64]{1,3,2,0:T(8,128)} fusion(f32[2,256,64,64]{1,3,2,0:T(8,128)} %get-tuple-element.638, s32[]{:T(128)S(6)} %copy.206, f32[64,256]{1,0:T(8,128)S(1)} %bitcast.234, f32[64,256]{1,0:T(8,128)S(1)} %get-tuple-element.606, f32[256,256]{1,0:T(8,128)S(1)} %fusion.80, ...), kind=kOutput, calls=%fused_computation.27.clone.1 | convolution fusion | flops 562036736 | bytes 6816768 | tf_op jit(solution)/shard_map/while/body/eval_jaxpr/hts,shp->thp/dot_general | solution.py:61
  154.5 1.9 copy-done.1
  157.7 7.9 %bitcast_dynamic-update-slice_fusion.8 = f32[2,256,64,64]{1,3,2,0:T(8,128)} fusion(f32[2,256,64,64]{1,3,2,0:T(8,128)} %get-tuple-element.638, s32[]{:T(128)S(6)} %copy.206, f32[64,256]{1,0:T(8,128)S(1)} %bitcast.234, f32[64,256]{1,0:T(8,128)S(1)} %get-tuple-element.606, f32[256,256]{1,0:T(8,128)S(1)} %fusion.80, ...), kind=kOutput, calls=%fused_computation.27.clone.1 | convolution fusion | flops 562036736 | bytes 6816768 | tf_op jit(solution)/shard_map/while/body/eval_jaxpr/hts,shp->thp/dot_general | solution.py:61
  166.8 1.9 copy-done.1
  168.9 3.9 while.55
  168.9 1.9 bitcast_add_fusion.8
  174.6 3.7 copy.158
  180.0 275.2 %all-to-all-done.3 = f32[8,4,16,64,128]{4,3,2,1,0:T(8,128)} async-done(((f32[8,4,16,64,128]{4,3,2,1,0:T(8,128)}), f32[8,4,16,64,128]{4,3,2,1,0:T(8,128)}, u32[]{:S(2)}, u32[]{:S(2)}) %all-to-all-start.3) | async-done | bytes 16777248 | tf_op jit(solution)/shard_map/all_to_all | solution.py:184
  455.2 9.6 %gather_fusion.6 = f32[13,16,64,128]{3,2,1,0:T(8,128)} fusion(f32[32,16,64,128]{3,2,1,0:T(8,128)} %bitcast.38, s32[1024]{0:T(1024)S(1)} %pad_clamp_fusion), kind=kCustom, calls=%fused_computation.6 | custom fusion | bytes 13631540 | tf_op jit(solution)/shard_map/jit(_take)/gather | solution.py:196
  464.8 7.4 %broadcast_select_fusion.3 = f32[13,16,64,128]{3,2,1,0:T(8,128)} fusion(f32[13,16,64,128]{3,2,1,0:T(8,128)} %gather_fusion.6, pred[13]{0:T(512)(128)(4,1)S(1)} %compare_and_fusion.2), kind=kLoop, calls=%fused_computation.92 | loop fusion | flops 1703936 | bytes 13631501 | tf_op jit(solution)/shard_map/jit(_take)/select_n | solution.py:196
  472.2 2.1 slice_bitcast_fusion
  477.1 8.7 %while.56 = (s32[]{:T(128)}, f32[1,64]{1,0:T(1,128)S(1)}, f32[1,64,64,128]{3,2,1,0:T(8,128)S(1)}, s32[]{:T(128)}, f32[4,1,64]{2,1,0:T(1,128)S(1)}, /*index=5*/f32[4,1,64,64,128]{4,3,2,1,0:T(8,128)}, s32[]{:T(128)}, s32[]{:T(128)}) while((s32[]{:T(128)}, f32[1,64]{1,0:T(1,128)S(1)}, f32[1,64,64,128]{3,2,1,0:T(8,128)S(1)}, ...), condition=%wide.region_17.18_spmd.clone, body=%wide.region_16.17_spmd.clone.sunk | while | flops 2097348 | bytes 6293119 | solution.py:37
  477.1 2.1 fusion.86
  479.2 2.2 fusion.86
  481.5 2.1 fusion.86
  483.7 2.1 fusion.86
  485.8 3.6 slice-done
  489.3 3.5 pad_maximum_fusion
  492.9 2.6 all-gather.5.cloned.1.call-done
  495.5 2.5 fusion.45
  498.0 9.0 %while.54 = (s32[]{:T(128)}, f32[1,64,64,128]{3,2,1,0:T(8,128)S(1)}, f32[2,1,256,64,64]{2,4,3,1,0:T(8,128)}, f32[2,1,256,64]{2,3,1,0:T(8,128)S(1)}, f32[2,1,64,6...) while((s32[]{:T(128)}, f32[1,64,64,128]{3,2,1,0:T(8,128)S(1)}, ...), condition=%wide.region_19.20_spmd, body=%wide.region_18.19_spmd.sunk | while | flops 1612709888 | bytes 29689720 | solution.py:121
  498.0 3.9 bitcast_dynamic-update-slice_fusion.11
  502.6 3.8 bitcast_dynamic-update-slice_fusion.11
  507.0 11.7 %bitcast_add_fusion.3 = f32[2,256,64,64]{1,3,2,0:T(8,128)} fusion(f32[2,256,64,64]{1,3,2,0:T(8,128)} %get-tuple-element.220, f32[2,1,256,64,64]{2,4,3,1,0:T(8,128)} %get-tuple-element.223), kind=kLoop, calls=%fused_computation.85 | loop fusion | flops 2097152 | bytes 25165824 | tf_op jit(solution)/shard_map/add | solution.py:134
  518.6 16.3 %copy.157 = f32[2,256,64,64]{3,2,1,0:T(8,128)} copy(f32[2,256,64,64]{1,3,2,0:T(8,128)} %bitcast_add_fusion.3) | data formatting | bytes 16777216 | tf_op jit(solution)/shard_map/reshape | solution.py:134
  534.9 14.8 %reshape.651 = f32[1,512,4096]{2,1,0:T(8,128)} reshape(f32[2,256,64,64]{3,2,1,0:T(8,128)} %copy.157) | data formatting | bytes 16777216 | tf_op jit(solution)/shard_map/reshape | solution.py:134
  549.6 8.5 %multiply_reduce_fusion = (f32[512]{0:T(512)S(1)}, f32[1,512,4096]{2,1,0:T(8,128)S(1)}) fusion(bf16[1,512,4096]{2,1,0:T(8,128)(2,1)} %param.31, f32[512]{0:T(512)S(1)} %copy-done.15, f32[1,512,4096]{2,1,0:T(8,128)} %reshape.651, bf16[1,512,4352]{2,1,0:T(8,128)(2,1)} %copy-done.6, f32[4096]{0:T(1024)S(1)} %mul.312), kind=kLoop, calls=%fused_computation.87 | loop fusion | flops 29359616 | bytes 25186304 | tf_op jit(solution)/shard_map/reduce_sum | solution.py:143
  558.1 3.5 multiply_convert_fusion.6
  (208 shorter events, 30.9 us)
Async XLA Ops:
  7.2 12.9 %copy-start.8 = (bf16[1,512,256]{2,1,0:T(8,128)(2,1)S(1)}, bf16[1,512,256]{2,1,0:T(8,128)(2,1)}, u32[]{:S(2)}) copy-start(bf16[1,512,256]{2,1,0:T(8,128)(2,1)} %param.30) | copy-start | bytes 786436
  7.2 19.8 %copy-start.20 = (s32[13]{0:T(128)S(1)}, s32[13]{0:T(128)}, u32[]{:S(2)}) copy-start(s32[13]{0:T(128)} %param.28) | copy-start | bytes 160
  10.2 51.2 %all-to-all-start = ((s32[8,1,4]{2,1,0:T(1,128)}), s32[8,1,4]{2,1,0:T(1,128)S(1)}, u32[]{:S(2)}, u32[]{:S(2)}) async-start(s32[8,1,4]{2,1,0:T(1,128)} %copy.129), calls=%async_computation | async-start | bytes 8192 | tf_op jit(solution)/shard_map/all_to_all | solution.py:187
  17.5 161.7 %reduce-scatter.12.cloned.1.call-start = ((), (), s32[]{:S(2)}) async-start(), calls=%async_computation.11 | async-start | bytes 163840
  20.1 2.1 copy-start.7
  22.2 84.2 %collective-permute-start = (bf16[1,3,4352]{2,1,0:T(4,128)(2,1)S(1)}, bf16[1,3,4352]{2,1,0:T(4,128)(2,1)S(1)}, u32[]{:S(2)}, u32[]{:S(2)}) collective-permute-start(bf16[1,3,4352]{2,1,0:T(4,128)(2,1)S(1)} %slice.127), channel_id=1, source_target_pairs={{0,1},{1,2},{2,3},{4,5},{5,6},{6,7},{8,9},{9,10},{10,11},{12,13},{... | collective-permute-start | bytes 78344 | tf_op jit(solution)/shard_map/ppermute | solution.py:20
  34.3 11.3 %copy-start.17 = (bf16[13,3,64]{2,0,1:T(8,128)(2,1)S(1)}, bf16[13,3,64]{2,0,1:T(8,128)(2,1)}, u32[]{:S(2)}) copy-start(bf16[13,3,64]{2,0,1:T(8,128)(2,1)} %param.26) | copy-start | bytes 14980
  46.3 12.6 %copy-start.9 = (bf16[13,3,1024]{2,0,1:T(8,128)(2,1)S(1)}, bf16[13,3,1024]{2,0,1:T(8,128)(2,1)}, u32[]{:S(2)}) copy-start(bf16[13,3,1024]{2,0,1:T(8,128)(2,1)} %param.25) | copy-start | bytes 239620
  46.3 14.3 %copy-start.21 = (f32[64]{0:T(128)S(1)}, f32[64]{0:T(128)}, u32[]{:S(2)}) copy-start(f32[64]{0:T(128)} %param.37) | copy-start | bytes 772
  46.3 30.8 %copy-start.11 = (bf16[1,512,64]{1,2,0:T(8,128)(2,1)S(1)}, bf16[1,512,64]{1,2,0:T(8,128)(2,1)}, u32[]{:S(2)}) copy-start(bf16[1,512,64]{1,2,0:T(8,128)(2,1)} %param.32) | copy-start | bytes 196612
  46.3 30.8 %copy-start.18 = (f32[64]{0:T(128)S(1)}, f32[64]{0:T(128)}, u32[]{:S(2)}) copy-start(f32[64]{0:T(128)} %param.36) | copy-start | bytes 772
  46.3 31.2 %copy-start.22 = (u32[32]{0:T(128)S(1)}, u32[32]{0:T(128)}, u32[]{:S(2)}) copy-start(u32[32]{0:T(128)} %constant.239) | copy-start | bytes 388
  61.4 12.3 %all-to-all-start.2 = ((bf16[8,2,384]{2,1,0:T(2,128)(2,1)}), bf16[8,2,384]{2,1,0:T(2,128)(2,1)S(1)}, u32[]{:S(2)}, u32[]{:S(2)}) async-start(bf16[8,2,384]{2,1,0:T(2,128)(2,1)} %reshape.672), calls=%async_computation.2 | async-start | bytes 24576 | tf_op jit(solution)/shard_map/all_to_all | solution.py:186
  67.1 11.7 %copy-start.14 = (f32[512]{0:T(512)}, f32[512]{0:T(512)S(1)}, u32[]{:S(2)}) copy-start(f32[512]{0:T(512)S(1)} %fusion.50) | copy-start | bytes 6148
  73.7 12.5 %all-to-all-start.1 = ((bf16[8,4,3,1024]{3,1,2,0:T(4,128)(2,1)}), bf16[8,4,3,1024]{3,1,2,0:T(4,128)(2,1)S(1)}, u32[]{:S(2)}, u32[]{:S(2)}) async-start(bf16[8,4,3,1024]{3,1,2,0:T(4,128)(2,1)} %copy_select_fusion), calls=%async_computation.1 | async-start | bytes 393216 | tf_op jit(solution)/shard_map/all_to_all | solution.py:185
  85.8 6.3 %copy-start.10 = (f32[4,4352]{1,0:T(4,128)S(1)}, f32[4,4352]{1,0:T(4,128)}, u32[]{:S(2)}) copy-start(f32[4,4352]{1,0:T(4,128)} %param.34) | copy-start | bytes 208900
  86.2 369.0 %all-to-all-start.3 = ((f32[8,4,16,64,128]{4,3,2,1,0:T(8,128)}), f32[8,4,16,64,128]{4,3,2,1,0:T(8,128)}, u32[]{:S(2)}, u32[]{:S(2)}) async-start(f32[8,4,16,64,128]{4,3,2,1,0:T(8,128)} %broadcast_select_fusion.2), calls=%async_computation.4 | async-start | bytes 33554432 | tf_op jit(solution)/shard_map/all_to_all | solution.py:184
  92.0 380.2 %reduce-scatter.8.cloned.1.call-start = ((), (), s32[]{:S(2)}) async-start(), calls=%async_computation.7 | async-start | bytes 2621440 | tf_op jit(solution)/shard_map/reduce_scatter | solution.py:279
  94.5 85.5 %copy-start.12 = (bf16[13,3,64]{2,1,0:T(4,128)(2,1)}, bf16[13,3,64]{2,1,0:T(4,128)(2,1)S(1)}, u32[]{:S(2)}) copy-start(bf16[13,3,64]{2,1,0:T(4,128)(2,1)S(1)} %select_convert_fusion.1) | copy-start | bytes 14980
  106.5 3.2 copy-start.13
  115.4 2.0 copy-start.6
  145.3 8.3 %copy-start = (f32[2,64,64,128]{3,2,1,0:T(8,128)S(1)}, f32[2,64,64,128]{3,2,1,0:T(8,128)}, u32[]{:S(2)}) copy-start(f32[2,64,64,128]{3,2,1,0:T(8,128)} %get-tuple-element.639) | copy-start | bytes 12582916 | tf_op jit(solution)/shard_map/while
  145.4 8.3 %copy-start.5 = (bf16[2,256,64,64]{1,3,2,0:T(8,128)(2,1)S(1)}, bf16[2,256,64,64]{1,3,2,0:T(8,128)(2,1)}, u32[]{:S(2)}) copy-start(bf16[2,256,64,64]{1,3,2,0:T(8,128)(2,1)} %get-tuple-element.652) | copy-start | bytes 12582916 | tf_op jit(solution)/shard_map/while
  154.4 2.0 copy-start.1
  157.7 8.3 %copy-start = (f32[2,64,64,128]{3,2,1,0:T(8,128)S(1)}, f32[2,64,64,128]{3,2,1,0:T(8,128)}, u32[]{:S(2)}) copy-start(f32[2,64,64,128]{3,2,1,0:T(8,128)} %get-tuple-element.639) | copy-start | bytes 12582916 | tf_op jit(solution)/shard_map/while
  157.7 8.3 %copy-start.5 = (bf16[2,256,64,64]{1,3,2,0:T(8,128)(2,1)S(1)}, bf16[2,256,64,64]{1,3,2,0:T(8,128)(2,1)}, u32[]{:S(2)}) copy-start(bf16[2,256,64,64]{1,3,2,0:T(8,128)(2,1)} %get-tuple-element.652) | copy-start | bytes 12582916 | tf_op jit(solution)/shard_map/while
  166.7 2.0 copy-start.1
  172.8 5.5 copy-start.3
  172.8 6.1 %copy-start.19 = (f32[64]{0:T(128)S(1)}, f32[64]{0:T(128)}, u32[]{:S(2)}) copy-start(f32[64]{0:T(128)} %param.38) | copy-start | bytes 772
  174.5 300.4 %reduce-scatter.10.cloned.1.call-start = ((), (), s32[]{:S(2)}) async-start(), calls=%async_computation.10 | async-start | bytes 2621440
  178.3 298.8 %all-gather.7.cloned.1.call-start = ((), (), s32[]{:S(2)}) async-start(), calls=%async_computation.9 | async-start | bytes 10485760 | tf_op jit(solution)/shard_map/all_gather | solution.py:25
  178.9 316.6 %all-gather.5.cloned.1.call-start = ((), (), s32[]{:S(2)}) async-start(), calls=%async_computation.8 | async-start | bytes 2621440 | tf_op jit(solution)/shard_map/all_gather | solution.py:242
  464.8 9.5 %slice-start.1 = ((bf16[13,3,64]{2,1,0:T(4,128)(2,1)}), bf16[12,3,64]{2,1,0:T(4,128)(2,1)S(1)}, s32[]{:S(2)}) async-start(bf16[13,3,64]{2,1,0:T(4,128)(2,1)} %copy-done.12), calls=%async_computation.13 | async-start | bytes 24576 | tf_op jit(solution)/shard_map/slice | solution.py:293
  485.8 7.1 %copy-start.4 = (f32[1,64,64,128]{3,2,1,0:T(8,128)}, f32[1,64,64,128]{3,2,1,0:T(8,128)S(1)}, u32[]{:S(2)}) copy-start(f32[1,64,64,128]{3,2,1,0:T(8,128)S(1)} %get-tuple-element.221) | copy-start | bytes 6291460
  485.8 3.6 slice-start
  498.0 4.1 copy-start.2
  502.5 4.0 copy-start.2
  534.9 14.8 %copy-start.15 = (f32[512]{0:T(512)S(1)}, f32[512]{0:T(512)}, u32[]{:S(2)}) copy-start(f32[512]{0:T(512)} %copy-done.14) | copy-start | bytes 6148
  549.6 8.5 %copy-start.16 = (f32[4096]{0:T(1024)S(1)}, f32[4096]{0:T(1024)}, u32[]{:S(2)}) copy-start(f32[4096]{0:T(1024)} %param.39) | copy-start | bytes 49156
Sparse Core Ops, SparseCore 0:
  27.0 22.0 reduce-scatter.11
  174.7 32.3 reduce-scatter.7
  209.6 31.1 reduce-scatter.9
  242.2 58.2 all-gather.6
  474.4 20.9 all-gather.4
where the time goes:
time: 570 us; the launch traced here: 568 us
  waiting for transfers between devices  285 us (50%)
  local copies, waits for them, and re-layouts  112 us (20%)
  other arithmetic  87.9 us (15%)
  matrix products  25.4 us (4%)
  starting transfers between devices  23.9 us (4%)
  blocking collectives  17.6 us (3%)
  between operations  15.7 us (3%)
    all_to_all x1, waiting for transfers between devices, migrate(): lax.all_to_all(send_states, 'req', split_axis=0, concat_axis=0, tiled=True)  275 us
    reshape x2, local copies, waits for them, and re-layouts, assemble(): (intra_part + inter_parts).reshape(value_rows.shape)  31 us
    unnamed x50, local copies, waits for them, and re-layouts  16 us
    dot_general x2, matrix products, block_local(): jnp.einsum('hts,shp->thp', weights, value_rows, preferred_element_type=jn...  15.9 us
    select_n x2, other arithmetic, packed(): taken_rows = jnp.take(source, source_slot, axis=0)  13.2 us
    another operation x1, local copies, waits for them, and re-layouts, to_items(): source.reshape((batch_size * block_count, BLOCK_LEN) + source.shape[2:])  12.6 us
    gather x3, local copies, waits for them, and re-layouts, packed(): taken_rows = jnp.take(source, source_slot, axis=0)  12.5 us
    add x1, other arithmetic, assemble(): intra_part + inter_parts  11.7 us
  transfers between devices with their start and end apart: 10, of which 4 were waited for; matrix products, arithmetic and copies ran while one was open for 25% of the time, Pallas kernels for 0%

commit v1 on v0

--- a/solution.py
+++ b/solution.py
@@ -1,6 +1,10 @@
+import functools
+
 import jax
 import jax.numpy as jnp
 from jax import lax
+from jax.experimental import pallas as pl
+from jax.experimental.pallas import tpu as pltpu
 from jax.sharding import PartitionSpec as P
 
 HEAD_DIM = 64
@@ -152,53 +156,160 @@
     return jax.vmap(pick_rows)(raw_rows, positions)
 
 
+def pack_kernel(source_ref, keep_ref, state_ref, out_ref):
+    keep = keep_ref[pl.program_id(0)].astype(jnp.float32)
+    out_ref[...] = (state_ref[...] * keep).astype(out_ref.dtype)
+
+
+def pack_states(states, source_slot, keep):
+    count = source_slot.shape[0]
+    rows, lanes = states.shape[1:]
+    return pl.pallas_call(
+        pack_kernel,
+        grid_spec=pltpu.PrefetchScalarGridSpec(
+            num_scalar_prefetch=2,
+            grid=(count,),
+            in_specs=[pl.BlockSpec((1, rows, lanes), lambda i, source, keep: (source[i], 0, 0))],
+            out_specs=pl.BlockSpec((1, rows, lanes), lambda i, source, keep: (i, 0, 0)),
+        ),
+        out_shape=jax.ShapeDtypeStruct((count, rows, lanes), jnp.bfloat16),
+        compiler_params=pltpu.CompilerParams(dimension_semantics=("arbitrary",)),
+        cost_estimate=pl.CostEstimate(
+            flops=count * rows * lanes, bytes_accessed=6 * count * rows * lanes, transcendentals=0
+        ),
+    )(source_slot, keep, states)
+
+
+def unpack_kernel(prefills, several, first_ref, later_ref, pick_ref, *refs):
+    final_ref, head_ref = refs[:2]
+    out_ref = refs[-1]
+    slot = pl.program_id(0)
+
+    @pl.when(slot < prefills)
+    def _():
+        out_ref[...] = final_ref[...]
+
+    @pl.when((slot >= prefills) & (pick_ref[slot] == 0))
+    def _():
+        out_ref[...] = head_ref[...].astype(out_ref.dtype)
+
+    if several:
+
+        @pl.when((slot >= prefills) & (pick_ref[slot] != 0))
+        def _():
+            out_ref[...] = refs[2][...].astype(out_ref.dtype)
+
+
+def unpack_states(final_own, head, rest, first, later, pick, slots):
+    prefills, rows, lanes = final_own.shape
+    block = (1, rows, lanes)
+    several = rest is not None
+    operands = [final_own, head] + ([rest] if several else [])
+    in_specs = [
+        pl.BlockSpec(block, lambda i, f, l, p: (jnp.minimum(i, prefills - 1), 0, 0)),
+        pl.BlockSpec(block, lambda i, f, l, p: (f[i], 0, 0)),
+    ]
+    if several:
+        in_specs.append(pl.BlockSpec(block, lambda i, f, l, p: (l[i], 0, 0)))
+    return pl.pallas_call(
+        functools.partial(unpack_kernel, prefills, several),
+        grid_spec=pltpu.PrefetchScalarGridSpec(
+            num_scalar_prefetch=3,
+            grid=(slots,),
+            in_specs=in_specs,
+            out_specs=pl.BlockSpec(block, lambda i, f, l, p: (i, 0, 0)),
+        ),
+        out_shape=jax.ShapeDtypeStruct((slots, rows, lanes), jnp.float32),
+        compiler_params=pltpu.CompilerParams(dimension_semantics=("arbitrary",)),
+        cost_estimate=pl.CostEstimate(
+            flops=slots * rows * lanes, bytes_accessed=6 * slots * rows * lanes, transcendentals=0
+        ),
+    )(first, later, pick, *operands)
+
+
+def held_forward(indices, used):
+    count = indices.shape[0]
+    order = jnp.arange(count, dtype=jnp.int32)
+    usable = used[None, :] & (order[None, :] <= order[:, None])
+    last_used = jnp.max(jnp.where(usable, order[None, :], -1), axis=1)
+    match = order[None, :] == last_used[:, None]
+    return jnp.sum(jnp.where(match, indices[None, :], 0), axis=1).astype(jnp.int32)
+
+
+def exchange(source):
+    return lax.all_to_all(source, "req", split_axis=0, concat_axis=0, tiled=True)
+
+
+def ranks_of(target_device, target_slot):
+    slot_count = target_slot.shape[-1]
+    slot_index = jnp.arange(slot_count, dtype=jnp.int32)
+    order = jnp.where(target_slot < PREFILLS, slot_index, slot_index + slot_count)
+    same = target_device[..., None, :] == target_device[..., :, None]
+    earlier = same & (order[..., None, :] < order[..., :, None])
+    return jnp.sum(earlier.astype(jnp.int32), axis=-1)
+
+
 def migrate(pool_states, inner_window, state_window, move_plan, active_mask):
     slot_count = pool_states.shape[0]
     peer_count = lax.axis_size("req")
     capacity = (2 * slot_count + peer_count - 1) // peer_count
     keep_flag = active_mask.astype(jnp.float32)
-    target_device = move_plan[:, 0]
-    target_slot = move_plan[:, 1]
     slot_index = jnp.arange(slot_count, dtype=jnp.int32)
-    earlier = (target_device[None, :] == target_device[:, None]) & (
-        slot_index[None, :] < slot_index[:, None]
-    )
-    send_rank = jnp.sum(earlier.astype(jnp.int32), axis=1)
-    matches = (target_device[None, None, :] == jnp.arange(peer_count)[:, None, None]) & (
-        send_rank[None, None, :] == jnp.arange(capacity)[None, :, None]
-    )
-    source_slot = jnp.sum(jnp.where(matches, slot_index[None, None, :], 0), axis=2).reshape(-1)
-    filled = jnp.any(matches, axis=2).reshape(-1)
-    slot_tags = jnp.where(filled, jnp.take(target_slot, source_slot), -1).reshape(
-        peer_count, capacity
-    )
-
-    def packed(source):
-        taken_rows = jnp.take(source, source_slot, axis=0)
-        return taken_rows.reshape((peer_count, capacity) + source.shape[1:])
-
-    send_states = packed(pool_states * keep_flag[:, None, None, None])
-    send_inner = packed(inner_window.astype(jnp.float32) * keep_flag[:, None, None])
-    send_outer = packed(state_window.astype(jnp.float32) * keep_flag[:, None, None])
-    got_states, got_inner, got_outer, got_tags = (
-        lax.all_to_all(send_states, "req", split_axis=0, concat_axis=0, tiled=True),
-        lax.all_to_all(send_inner, "req", split_axis=0, concat_axis=0, tiled=True),
-        lax.all_to_all(send_outer, "req", split_axis=0, concat_axis=0, tiled=True),
-        lax.all_to_all(slot_tags, "req", split_axis=0, concat_axis=0, tiled=True),
-    )
-    flat_tags = got_tags.reshape(-1)
-    arrivals = jnp.arange(flat_tags.shape[0], dtype=jnp.int32)
-    chosen = jnp.sum(
-        jnp.where(flat_tags[None, :] == slot_index[:, None], arrivals[None, :], 0), axis=1
-    )
-
-    def placed(source):
-        return jnp.take(source.reshape((-1,) + source.shape[2:]), chosen, axis=0)
+    send_rank = ranks_of(move_plan[:, 0], move_plan[:, 1])
+    peers = jnp.arange(peer_count)
+    matches = (move_plan[:, 0][None, None, :] == peers[None, :, None]) & (
+        send_rank[None, None, :] == jnp.arange(capacity)[:, None, None]
+    )
+    source_slot = jnp.sum(jnp.where(matches, slot_index[None, None, :], 0), axis=2)
+    filled = jnp.any(matches, axis=2)
+    every_plan = lax.all_gather(move_plan, "req")
+    every_rank = ranks_of(every_plan[..., 0], every_plan[..., 1])
+    mine = every_plan[..., 0] == lax.axis_index("req")
+    hits = (mine[..., None] & (every_plan[..., 1][..., None] == slot_index)).astype(jnp.int32)
+    from_peer = jnp.sum(hits * peers[:, None, None], axis=(0, 1)).astype(jnp.int32)
+    from_rank = jnp.sum(hits * every_rank[..., None], axis=(0, 1)).astype(jnp.int32)
+
+    windows = jnp.concatenate([inner_window, state_window], axis=2)
+    windows = (windows.astype(jnp.float32) * keep_flag[:, None, None]).astype(jnp.bfloat16)
+    send_windows = jnp.take(windows, source_slot.T.reshape(-1), axis=0)
+    got_windows = exchange(send_windows.reshape((peer_count, capacity) + windows.shape[1:]))
+    got_windows = got_windows.reshape((-1,) + windows.shape[1:])
+    moved_windows = jnp.take(got_windows, from_peer * capacity + from_rank, axis=0)
+
+    flat_states = pool_states.reshape(slot_count, -1, pool_states.shape[-1])
+
+    def sent(low, high):
+        part, used = source_slot[low:high].T.reshape(-1), filled[low:high].T.reshape(-1)
+        keep = jnp.sum(
+            jnp.where(part[:, None] == slot_index[None, :], active_mask[None, :], 0), axis=1
+        )
+        packed = pack_states(flat_states, held_forward(part, used), keep.astype(jnp.int32))
+        return packed.reshape((peer_count, high - low) + packed.shape[1:])
+
+    head = exchange(sent(0, 1)).reshape((peer_count,) + flat_states.shape[1:])
+    rest = None
+    if capacity > 1:
+        later_send = sent(1, capacity)
+        later_send, head = lax.optimization_barrier((later_send, head))
+        rest = exchange(later_send).reshape((-1,) + flat_states.shape[1:])
+    in_head = from_rank == 0
+    first = held_forward(from_peer, in_head)
+    later = held_forward(from_peer * max(1, capacity - 1) + from_rank - 1, ~in_head)
+    pick = from_rank
+    initial_own = lax.dynamic_index_in_dim(head, from_peer[0], 0, keepdims=True)
+    initial_own = initial_own.astype(jnp.float32).reshape((PREFILLS,) + pool_states.shape[1:])
+    inner_width = inner_window.shape[2]
+
+    def place(final_own):
+        final_rows = final_own.reshape((PREFILLS,) + flat_states.shape[1:])
+        placed = unpack_states(final_rows, head, rest, first, later, pick, slot_count)
+        return placed.reshape(pool_states.shape)
 
     return (
-        placed(got_states),
-        placed(got_inner).astype(jnp.bfloat16),
-        placed(got_outer).astype(jnp.bfloat16),
+        initial_own,
+        place,
+        moved_windows[:, :, :inner_width],
+        moved_windows[:, :, inner_width:],
     )
 
 
@@ -227,19 +338,19 @@
     skip_weight,
     norm_weight,
 ):
-    moved_states, moved_inner, moved_outer = migrate(
+    initial_own, place, moved_inner, moved_outer = migrate(
         pool_states, inner_window, state_window, move_plan, active_mask
     )
     chain_index = lax.axis_index("seq")
     chain_size = lax.axis_size("seq")
     local_length = inputs_inner.shape[1]
-    local_heads = moved_states.shape[1]
+    local_heads = initial_own.shape[1]
     decay_rates = -jnp.exp(decay_log)
     offsets = jnp.arange(KERNEL - 1, dtype=jnp.int32)
     raw_rows = jnp.concatenate([inputs_inner, inputs_state], axis=2)
     earlier_rows = shifted(raw_rows[:, local_length - KERNEL + 1 :], "seq", 1)
     initial, head_inner, head_outer = (
-        lax.all_gather(moved_states[:PREFILLS], "seq", axis=1, tiled=True),
+        lax.all_gather(initial_own, "seq", axis=1, tiled=True),
         lax.all_gather(moved_inner[:PREFILLS].astype(jnp.float32), "seq", axis=2, tiled=True),
         lax.all_gather(moved_outer[:PREFILLS].astype(jnp.float32), "seq", axis=2, tiled=True),
     )
@@ -283,12 +394,12 @@
         lax.psum_scatter(window_term[:, :, INNER_DIM:], "seq", scatter_dimension=2, tiled=True),
     )
     own_decay = lax.dynamic_slice_in_dim(whole_decay, chain_index * local_heads, local_heads, 1)
-    final_own = state_sum + own_decay[:, :, None, None] * moved_states[:PREFILLS]
+    final_own = state_sum + own_decay[:, :, None, None] * initial_own
     kept_inner = inner_sum.astype(jnp.bfloat16)
     kept_outer = outer_sum.astype(jnp.bfloat16)
     mixer_rows = assemble(intra_part, inter_parts, value_rows, skip_weight, valid_rows)
     mixer_out = gated_norm(mixer_rows, gate_rows, norm_weight)
-    new_states = jnp.concatenate([final_own, moved_states[PREFILLS:]], axis=0)
+    new_states = place(final_own)
     new_inner = jnp.concatenate([kept_inner, moved_inner[PREFILLS:]], axis=0)
     new_outer = jnp.concatenate([kept_outer, moved_outer[PREFILLS:]], axis=0)
     return (new_states, new_inner, new_outer, mixer_out)

time: 570 us -> 364 us (0.64)
  waiting for transfers between devices: 285 us -> 87.7 us
  Pallas kernels: 0 us -> 29.3 us
  local copies, waits for them, and re-layouts: 112 us -> 83.8 us
  other arithmetic: 87.9 us -> 62.1 us
  blocking collectives: 17.6 us -> 38.6 us
  starting transfers between devices: 23.9 us -> 17.8 us
    all_to_all x4 -> x3, waiting for transfers between devices: 282 us -> 60.4 us  [exchange(): lax.all_to_all(source, 'req', split_axis=0, concat_axis=0, tiled=True)]
    pallas_call x0 -> x3, Pallas kernels: none -> 29.3 us  [the longest x2 19.3 us: pack_states(): pl.pallas_call(pack_kernel, grid_spec=pltpu.PrefetchScalarGridSpec(num_sc...]
    gather x9 -> x2, local copies, waits for them, and re-layouts: 24.2 us -> 1.47 us  [the longest x1 0.82 us: migrate(): send_windows = jnp.take(windows, source_slot.T.reshape(-1), axis=0)]
    all_gather x0 -> x1, blocking collectives: none -> 21 us  [migrate(): every_plan = lax.all_gather(move_plan, 'req')]
    select_n x6, other arithmetic: 20.7 us -> 1.01 us  [the longest x2 0.87 us: migrate(): send_windows = jnp.take(windows, source_slot.T.reshape(-1), axis=0)]
    all_gather x1, waiting for transfers between devices: 2.59 us -> 15.3 us  [on_device(): lax.all_gather(initial_own, 'seq', axis=1, tiled=True)]
    all_gather x1, waiting for transfers between devices: 0.01 us -> 11.7 us  [entering(): everything = jax.tree.map(lambda part: lax.all_gather(part, axis), shard)]
    mul x3 -> x0, other arithmetic: 7.54 us -> none  [the longest x1 7.39 us: migrate(): send_states = packed(pool_states * keep_flag[:, None, None, None])]
  transfers between devices with their start and end apart: 10 -> 9, of which waited for: 4 -> 4; matrix products, arithmetic and copies ran while one was open for 25% -> 44% of each run, Pallas kernels for 0% -> 5%
where the time goes in v1:
time: 364 us; the launch traced here: 361 us
  waiting for transfers between devices  87.7 us (24%)
  local copies, waits for them, and re-layouts  83.8 us (23%)
  other arithmetic  62.1 us (17%)
  blocking collectives  38.6 us (11%)
  Pallas kernels  29.3 us (8%)
  matrix products  25.2 us (7%)
  starting transfers between devices  17.8 us (5%)
  between operations  15.9 us (4%)
    all_to_all x3, waiting for transfers between devices, exchange(): lax.all_to_all(source, 'req', split_axis=0, concat_axis=0, tiled=True)  60.4 us
    reshape x2, local copies, waits for them, and re-layouts, assemble(): (intra_part + inter_parts).reshape(value_rows.shape)  31 us
    all_gather x1, blocking collectives, migrate(): every_plan = lax.all_gather(move_plan, 'req')  21 us
    pallas_call x2, Pallas kernels, pack_states(): pl.pallas_call(pack_kernel, grid_spec=pltpu.PrefetchScalarGridSpec(num_sc...  19.3 us
    dot_general x2, matrix products, block_local(): jnp.einsum('hts,shp->thp', weights, value_rows, preferred_element_type=jn...  15.9 us
    unnamed x54, local copies, waits for them, and re-layouts  15.4 us
    all_gather x1, waiting for transfers between devices, on_device(): lax.all_gather(initial_own, 'seq', axis=1, tiled=True)  15.3 us
    all_to_all x3, starting transfers between devices, exchange(): lax.all_to_all(source, 'req', split_axis=0, concat_axis=0, tiled=True)  15 us
  transfers between devices with their start and end apart: 9, of which 4 were waited for; matrix products, arithmetic and copies ran while one was open for 44% of the time, Pallas kernels for 5%

profile of v1, /device:TPU:0, one launch (start us, length us, event | category | flops | bytes accessed | tf_op | source)
XLA Modules:
  0.0 361.0 jit_solution(6218070920709365392)
XLA Ops:
  7.3 2.6 constant_dynamic-update-slice_fusion.1
  10.0 2.1 copy-done.7
  12.1 2.4 collective-permute-start
  15.2 1.6 gather_fusion.2
  20.3 6.6 %all-to-all-start = ((bf16[8,4,3,1088]{3,1,2,0:T(4,128)(2,1)}), bf16[8,4,3,1088]{3,1,2,0:T(4,128)(2,1)S(1)}, u32[]{:S(2)}, u32[]{:S(2)}) async-start(bf16[8,4,3,1088]{3,1,2,0:T(4,128)(2,1)} %copy_select_fusion), calls=%async_computation | async-start | bytes 442368 | tf_op jit(solution)/shard_map/all_to_all | solution.py:240
  27.0 3.7 %copy.136 = f32[1,3,4096]{1,0,2:T(1,128)} copy(f32[1,3,4096]{2,1,0:T(4,128)S(1)} %slice.155) | data formatting | bytes 98304
  30.8 21.0 %all-gather.3 = s32[8,13,2]{1,2,0:T(2,128)S(1)} all-gather(s32[1,13,2]{1,2,0:T(2,128)S(1)} %bitcast.283), channel_id=2, replica_groups=mesh['req'=8,'seq'=4] {'req'}, dimensions={0}, use_global_device_ids=true | all-gather | bytes 936 | tf_op jit(solution)/shard_map/all_gather | solution.py:265
  53.8 5.6 %all-reduce = f32[256]{0:T(256)S(1)} all-reduce(f32[256]{0:T(256)S(1)} %exponential_dynamic-update-slice_fusion), channel_id=3, replica_groups=mesh['req'=8,'seq'=4] {'seq'}, use_global_device_ids=true, to_apply=%add | all-reduce | flops 256 | bytes 2048
  61.6 6.4 %all_gather.29 = bf16[1,3,256]{1,0,2:T(2,128)(2,1)S(1)} all-gather(bf16[1,3,64]{1,0,2:T(2,128)(2,1)S(1)} %copy.114), channel_id=1, replica_groups=mesh['req'=8,'seq'=4] {'seq'}, dimensions={2}, use_global_device_ids=true | all-gather | bytes 1920 | tf_op jit(solution)/shard_map/all_gather | solution.py:355
  68.0 5.7 %all_gather.28 = bf16[1,3,4096]{2,1,0:T(4,128)(2,1)S(1)} all-gather(bf16[1,3,1024]{2,1,0:T(4,128)(2,1)S(1)} %slice.209), channel_id=1, replica_groups=mesh['req'=8,'seq'=4] {'seq'}, dimensions={2}, use_global_device_ids=true | all-gather | bytes 30720 | tf_op jit(solution)/shard_map/all_gather | solution.py:354
  73.7 3.2 maximum_convert_fusion
  77.0 5.7 %multiply_convert_fusion.5 = bf16[1,512,4352]{2,1,0:T(8,128)(2,1)S(1)} fusion(f32[1,515,4352]{2,1,0:T(8,128)S(1)} %maximum_convert_fusion, f32[4352]{0:T(1024)S(1)} %get-tuple-element.373, f32[4352]{0:T(1024)S(1)} %get-tuple-element.374, f32[4352]{0:T(1024)S(1)} %get-tuple-element.372, f32[4352]{0:T(1024)S(1)} %get-tuple-element.371, f32[4352]{0:T(1024)S(1)} %copy-done.13), kind=kLoop, calls=%fused_computation.75 | loop fusion | flops 28966912 | bytes 40195072 | tf_op jit(solution)/shard_map/convert_element_type | solution.py:50
  82.7 2.9 slice.152
  86.2 12.6 %reshape.688 = bf16[2,256,64,64]{3,2,1,0:T(8,128)(2,1)} reshape(bf16[1,512,4096]{2,1,0:T(8,128)(2,1)} %slice.152) | data formatting | bytes 8388608 | tf_op jit(solution)/shard_map/reshape;reshape | solution.py:77
  98.7 10.5 %copy.117 = bf16[2,256,64,64]{1,3,2,0:T(8,128)(2,1)} copy(bf16[2,256,64,64]{3,2,1,0:T(8,128)(2,1)} %reshape.688) | data formatting | bytes 8388608 | tf_op jit(solution)/shard_map/while | solution.py:85
  109.2 24.6 %while.53 = (s32[]{:T(128)}, f32[2,256,64,64]{1,3,2,0:T(8,128)}, f32[2,64,64,128]{3,2,1,0:T(8,128)}, f32[2,256,64]{1,2,0:T(8,128)S(1)}, bf16[2,256,64,64]{1,3,2,...) while((s32[]{:T(128)}, f32[2,256,64,64]{1,3,2,0:T(8,128)}, ...), condition=%wide.region_12.13_spmd, body=%wide.region_9.12_spmd.sunk | while | flops 852639936 | bytes 62990296 | solution.py:85
  110.5 7.9 %bitcast_dynamic-update-slice_fusion.8 = f32[2,256,64,64]{1,3,2,0:T(8,128)} fusion(f32[2,256,64,64]{1,3,2,0:T(8,128)} %get-tuple-element.624, s32[]{:T(128)S(6)} %copy.183, f32[64,256]{1,0:T(8,128)S(1)} %bitcast.266, f32[64,256]{1,0:T(8,128)S(1)} %get-tuple-element.592, f32[256,256]{1,0:T(8,128)S(1)} %fusion.87, ...), kind=kOutput, calls=%fused_computation.22.clone.1 | convolution fusion | flops 562036736 | bytes 6816768 | tf_op jit(solution)/shard_map/while/body/eval_jaxpr/hts,shp->thp/dot_general | solution.py:65
  119.6 1.9 copy-done.1
  122.9 7.9 %bitcast_dynamic-update-slice_fusion.8 = f32[2,256,64,64]{1,3,2,0:T(8,128)} fusion(f32[2,256,64,64]{1,3,2,0:T(8,128)} %get-tuple-element.624, s32[]{:T(128)S(6)} %copy.183, f32[64,256]{1,0:T(8,128)S(1)} %bitcast.266, f32[64,256]{1,0:T(8,128)S(1)} %get-tuple-element.592, f32[256,256]{1,0:T(8,128)S(1)} %fusion.87, ...), kind=kOutput, calls=%fused_computation.22.clone.1 | convolution fusion | flops 562036736 | bytes 6816768 | tf_op jit(solution)/shard_map/while/body/eval_jaxpr/hts,shp->thp/dot_general | solution.py:65
  131.9 1.9 copy-done.1
  134.0 3.9 %while.55 = (s32[]{:T(128)}, f32[1,64,64,128]{3,2,1,0:T(8,128)S(1)}, f32[2,1,256,64]{3,2,1,0:T(8,128)S(1)}, f32[2,1,64,64,128]{4,3,2,1,0:T(8,128)}, s32[]{:T(128)}, /*index=5*/s32[]{:T(128)}) while((s32[]{:T(128)}, f32[1,64,64,128]{3,2,1,0:T(8,128)S(1)}, f32[2,1,256,64]{3,2,1,0:T(8,128)S(1)}, f32[2,1,64,64,128]{4,3,2,1,0:T(8,128)}, ...), condition=%wide.region_14.15_spmd.clone, body=%wide.region_13.14_spmd.clone.sunk | while | flops 1572867 | bytes 6423391 | solution.py:103
  134.0 1.9 bitcast_add_fusion.8
  136.0 1.9 bitcast_add_fusion.8
  137.9 1.7 broadcast_multiply_fusion
  141.9 6.0 %shard_map.184 = bf16[8,1024,128]{2,1,0:T(8,128)(2,1)} custom-call(s32[8]{0:T(128)} %select_reduce_fusion.10.source_ref, s32[8]{0:T(128)} %select_reduce_fusion.9.keep_ref, f32[13,1024,128]{2,1,0:T(8,128)} %bitcast.250), custom_call_target="tpu_custom_call" | custom-call | flops 1048576 | bytes 6291456 | tf_op jit(solution)/shard_map/pallas_call | solution.py:167
  148.0 3.6 all-to-all-start.1
  153.4 13.3 %shard_map.183 = bf16[24,1024,128]{2,1,0:T(8,128)(2,1)} custom-call(s32[24]{0:T(128)} %select_reduce_fusion.2.source_ref, s32[24]{0:T(128)} %select_reduce_fusion.4.keep_ref, f32[13,1024,128]{2,1,0:T(8,128)} %bitcast.251), custom_call_target="tpu_custom_call" | custom-call | flops 3145728 | bytes 18874368 | tf_op jit(solution)/shard_map/pallas_call | solution.py:167
  166.6 33.8 %all-to-all-done.1 = bf16[8,1,1024,128]{3,2,1,0:T(8,128)(2,1)S(1)} async-done(((bf16[8,1,1024,128]{3,2,1,0:T(8,128)(2,1)}), bf16[8,1,1024,128]{3,2,1,0:T(8,128)(2,1)S(1)}, u32[]{:S(2)}, u32[]{:S(2)}) %all-to-all-start.1) | async-done | bytes 2097184 | tf_op jit(solution)/shard_map/all_to_all | solution.py:240
  201.8 4.8 %all-to-all-start.2 = ((bf16[8,3,1024,128]{3,2,1,0:T(8,128)(2,1)}), bf16[8,3,1024,128]{3,2,1,0:T(8,128)(2,1)}, u32[]{:S(2)}, u32[]{:S(2)}) async-start(bf16[8,3,1024,128]{3,2,1,0:T(8,128)(2,1)} %bitcast.252), calls=%async_computation.3 | async-start | bytes 12582912 | tf_op jit(solution)/shard_map/all_to_all | solution.py:240
  214.3 2.0 fusion.46
  216.3 11.7 %all-gather.9.cloned.1.call-done = f32[4,64,64,128]{3,2,1,0:T(8,128)} async-done(((f32[1,64,64,128]{3,2,1,0:T(8,128)}), f32[4,64,64,128]{3,2,1,0:T(8,128)}) %all-gather.9.cloned.1.call-update) | async-done | bytes 8388624 | tf_op jit(solution)/shard_map/all_gather | solution.py:29
  227.9 8.7 %while.56 = (s32[]{:T(128)}, f32[1,64]{1,0:T(1,128)S(1)}, f32[1,64,64,128]{3,2,1,0:T(8,128)S(1)}, s32[]{:T(128)}, f32[4,1,64]{2,1,0:T(1,128)S(1)}, /*index=5*/f32[4,1,64,64,128]{4,3,2,1,0:T(8,128)}, s32[]{:T(128)}, s32[]{:T(128)}) while((s32[]{:T(128)}, f32[1,64]{1,0:T(1,128)S(1)}, f32[1,64,64,128]{3,2,1,0:T(8,128)S(1)}, ...), condition=%wide.region_29.30_spmd.clone, body=%wide.region_28.29_spmd.clone.sunk | while | flops 2097348 | bytes 6293119 | solution.py:41
  227.9 2.1 fusion.93
  230.1 2.1 fusion.93
  232.2 2.1 fusion.93
  234.4 2.2 fusion.93
  236.6 15.3 %all-gather.7.cloned.1.call-done = f32[1,64,64,128]{3,2,0,1:T(8,128)} async-done(((f32[1,16,64,128]{3,2,0,1:T(8,128)}), f32[1,64,64,128]{3,2,0,1:T(8,128)}) %all-gather.7.cloned.1.call-update) | async-done | bytes 2097168 | tf_op jit(solution)/shard_map/all_gather | solution.py:353
  251.9 2.5 fusion.45
  254.4 8.9 %while.54 = (s32[]{:T(128)}, f32[1,64,64,128]{3,2,1,0:T(8,128)S(1)}, f32[2,1,256,64,64]{2,4,3,1,0:T(8,128)}, f32[2,1,256,64]{2,3,1,0:T(8,128)S(1)}, f32[2,1,64,6...) while((s32[]{:T(128)}, f32[1,64,64,128]{3,2,1,0:T(8,128)S(1)}, ...), condition=%wide.region_31.32_spmd, body=%wide.region_30.31_spmd.sunk | while | flops 1612709888 | bytes 29689720 | solution.py:125
  254.5 3.7 %bitcast_dynamic-update-slice_fusion.11 = f32[2,1,256,64,64]{2,4,3,1,0:T(8,128)} fusion(f32[2,1,256,64,64]{2,4,3,1,0:T(8,128)} %get-tuple-element.696, s32[]{:T(128)S(6)} %copy.210, f32[1,64,64,128]{3,2,1,0:T(8,128)S(1)} %get-tuple-element.695, f32[256,64]{0,1:T(8,128)S(1)} %get-tuple-element.601, bf16[2,1,256,128]{3,2,1,0:T(8,128)(2,1)S(1)} %get-tuple-element.706), kind=kOutput, calls=%fused_computation.55.clone.1 | convolution fusion | flops 1611661312 | bytes 6423552 | tf_op jit(solution)/shard_map/while/body/eval_jaxpr/bqn,bhpn->bqhp/dot_general | solution.py:114
  258.9 3.8 %bitcast_dynamic-update-slice_fusion.11 = f32[2,1,256,64,64]{2,4,3,1,0:T(8,128)} fusion(f32[2,1,256,64,64]{2,4,3,1,0:T(8,128)} %get-tuple-element.696, s32[]{:T(128)S(6)} %copy.210, f32[1,64,64,128]{3,2,1,0:T(8,128)S(1)} %get-tuple-element.695, f32[256,64]{0,1:T(8,128)S(1)} %get-tuple-element.601, bf16[2,1,256,128]{3,2,1,0:T(8,128)(2,1)S(1)} %get-tuple-element.706), kind=kOutput, calls=%fused_computation.55.clone.1 | convolution fusion | flops 1611661312 | bytes 6423552 | tf_op jit(solution)/shard_map/while/body/eval_jaxpr/bqn,bhpn->bqhp/dot_general | solution.py:114
  263.3 11.7 %bitcast_add_fusion.3 = f32[2,256,64,64]{1,3,2,0:T(8,128)} fusion(f32[2,256,64,64]{1,3,2,0:T(8,128)} %get-tuple-element.224, f32[2,1,256,64,64]{2,4,3,1,0:T(8,128)} %get-tuple-element.227), kind=kLoop, calls=%fused_computation.80 | loop fusion | flops 2097152 | bytes 25165824 | tf_op jit(solution)/shard_map/add | solution.py:138
  275.0 16.3 %copy.135 = f32[2,256,64,64]{3,2,1,0:T(8,128)} copy(f32[2,256,64,64]{1,3,2,0:T(8,128)} %bitcast_add_fusion.3) | data formatting | bytes 16777216 | tf_op jit(solution)/shard_map/reshape | solution.py:138
  291.3 14.8 %reshape.689 = f32[1,512,4096]{2,1,0:T(8,128)} reshape(f32[2,256,64,64]{3,2,1,0:T(8,128)} %copy.135) | data formatting | bytes 16777216 | tf_op jit(solution)/shard_map/reshape | solution.py:138
  306.0 8.5 %multiply_reduce_fusion = (f32[512]{0:T(512)S(1)}, f32[1,512,4096]{2,1,0:T(8,128)S(1)}) fusion(bf16[1,512,4096]{2,1,0:T(8,128)(2,1)} %param.31, f32[512]{0:T(512)S(1)} %copy-done.15, f32[1,512,4096]{2,1,0:T(8,128)} %reshape.689, bf16[1,512,4352]{2,1,0:T(8,128)(2,1)} %copy-done.6, f32[4096]{0:T(1024)S(1)} %mul.342), kind=kLoop, calls=%fused_computation.82 | loop fusion | flops 29359616 | bytes 25186304 | tf_op jit(solution)/shard_map/reduce_sum | solution.py:147
  314.5 3.5 multiply_convert_fusion.6
  318.0 26.5 %all-to-all-done.2 = bf16[8,3,1024,128]{3,2,1,0:T(8,128)(2,1)} async-done(((bf16[8,3,1024,128]{3,2,1,0:T(8,128)(2,1)}), bf16[8,3,1024,128]{3,2,1,0:T(8,128)(2,1)}, u32[]{:S(2)}, u32[]{:S(2)}) %all-to-all-start.2) | async-done | bytes 6291488 | tf_op jit(solution)/shard_map/all_to_all | solution.py:240
  344.5 10.0 %shard_map.185 = f32[13,1024,128]{2,1,0:T(8,128)} custom-call(s32[13]{0:T(128)} %select_reduce_fusion.7.first_ref, s32[13]{0:T(128)} %select_reduce_fusion.5.later_ref, s32[13]{0:T(128)} %copy-done.18, f32[1,1024,128]{2,1,0:T(8,128)} %bitcast.265, bf16[8,1024,128]{2,1,0:T(8,128)(2,1)} %bitcast.255, bf16[24,1024,128]{2,1,0:T(8,128)(2,1)} %bitcast.52.refs_2_), custom_call_target="tpu_custom_call" | custom-call | flops 1703936 | bytes 10223616 | tf_op jit(solution)/shard_map/pallas_call | solution.py:214
  (220 shorter events, 26.8 us)
Async XLA Ops:
  7.2 2.7 copy-start.9
  7.2 10.5 %copy-start.19 = (s32[13,2]{0,1:T(2,128)S(1)}, s32[13,2]{0,1:T(2,128)}, u32[]{:S(2)}) copy-start(s32[13,2]{0,1:T(2,128)} %param.27) | copy-start | bytes 316
  7.2 10.5 %copy-start.17 = (bf16[13,3,64]{2,0,1:T(8,128)(2,1)S(1)}, bf16[13,3,64]{2,0,1:T(8,128)(2,1)}, u32[]{:S(2)}) copy-start(bf16[13,3,64]{2,0,1:T(8,128)(2,1)} %param.26) | copy-start | bytes 14980
  7.2 10.5 %copy-start.10 = (bf16[13,3,1024]{2,0,1:T(8,128)(2,1)S(1)}, bf16[13,3,1024]{2,0,1:T(8,128)(2,1)}, u32[]{:S(2)}) copy-start(bf16[13,3,1024]{2,0,1:T(8,128)(2,1)} %param.25) | copy-start | bytes 239620
  7.2 10.6 %copy-start.23 = (s32[13]{0:T(128)S(1)}, s32[13]{0:T(128)}, u32[]{:S(2)}) copy-start(s32[13]{0:T(128)} %param.28) | copy-start | bytes 160
  7.2 201.6 %reduce-scatter.12.cloned.1.call-start = ((), (), s32[]{:S(2)}) async-start(), calls=%async_computation.10 | async-start | bytes 163840
  9.9 42.3 %copy-start.22 = (f32[64]{0:T(128)S(1)}, f32[64]{0:T(128)}, u32[]{:S(2)}) copy-start(f32[64]{0:T(128)} %param.37) | copy-start | bytes 772
  9.9 42.3 %copy-start.24 = (u32[32]{0:T(128)S(1)}, u32[32]{0:T(128)}, u32[]{:S(2)}) copy-start(u32[32]{0:T(128)} %constant.201) | copy-start | bytes 388
  9.9 43.5 %copy-start.12 = (bf16[1,512,64]{1,2,0:T(8,128)(2,1)S(1)}, bf16[1,512,64]{1,2,0:T(8,128)(2,1)}, u32[]{:S(2)}) copy-start(bf16[1,512,64]{1,2,0:T(8,128)(2,1)} %param.32) | copy-start | bytes 196612
  9.9 43.5 %copy-start.20 = (f32[64]{0:T(128)S(1)}, f32[64]{0:T(128)}, u32[]{:S(2)}) copy-start(f32[64]{0:T(128)} %param.36) | copy-start | bytes 772
  9.9 50.4 %copy-start.11 = (f32[4,4352]{1,0:T(4,128)S(1)}, f32[4,4352]{1,0:T(4,128)}, u32[]{:S(2)}) copy-start(f32[4,4352]{1,0:T(4,128)} %param.34) | copy-start | bytes 208900
  10.0 2.1 copy-start.7
  12.1 61.6 %collective-permute-start = (bf16[1,3,4352]{2,1,0:T(4,128)(2,1)S(1)}, bf16[1,3,4352]{2,1,0:T(4,128)(2,1)S(1)}, u32[]{:S(2)}, u32[]{:S(2)}) collective-permute-start(bf16[1,3,4352]{2,1,0:T(4,128)(2,1)S(1)} %slice.147), channel_id=1, source_target_pairs={{0,1},{1,2},{2,3},{4,5},{5,6},{6,7},{8,9},{9,10},{10,11},{12,13},{... | collective-permute-start | bytes 78344 | tf_op jit(solution)/shard_map/ppermute | solution.py:24
  20.3 40.2 %all-to-all-start = ((bf16[8,4,3,1088]{3,1,2,0:T(4,128)(2,1)}), bf16[8,4,3,1088]{3,1,2,0:T(4,128)(2,1)S(1)}, u32[]{:S(2)}, u32[]{:S(2)}) async-start(bf16[8,4,3,1088]{3,1,2,0:T(4,128)(2,1)} %copy_select_fusion), calls=%async_computation | async-start | bytes 442368 | tf_op jit(solution)/shard_map/all_to_all | solution.py:240
  26.9 182.7 %reduce-scatter.10.cloned.1.call-start = ((), (), s32[]{:S(2)}) async-start(), calls=%async_computation.9 | async-start | bytes 2621440
  30.7 183.6 %reduce-scatter.8.cloned.1.call-start = ((), (), s32[]{:S(2)}) async-start(), calls=%async_computation.6 | async-start | bytes 2621440 | tf_op jit(solution)/shard_map/reduce_scatter | solution.py:390
  52.1 1.7 copy-start.14
  60.0 148.0 %copy-start.18 = (s32[13]{0:T(128)}, s32[13]{0:T(128)S(1)}, u32[]{:S(2)}) copy-start(s32[13]{0:T(128)S(1)} %get-tuple-element.375.pick_ref) | copy-start | bytes 160
  73.7 3.2 copy-start.13
  82.7 3.4 copy-start.6
  110.5 8.3 %copy-start = (f32[2,64,64,128]{3,2,1,0:T(8,128)S(1)}, f32[2,64,64,128]{3,2,1,0:T(8,128)}, u32[]{:S(2)}) copy-start(f32[2,64,64,128]{3,2,1,0:T(8,128)} %get-tuple-element.625) | copy-start | bytes 12582916 | tf_op jit(solution)/shard_map/while
  110.5 8.3 %copy-start.5 = (bf16[2,256,64,64]{1,3,2,0:T(8,128)(2,1)S(1)}, bf16[2,256,64,64]{1,3,2,0:T(8,128)(2,1)}, u32[]{:S(2)}) copy-start(bf16[2,256,64,64]{1,3,2,0:T(8,128)(2,1)} %get-tuple-element.638) | copy-start | bytes 12582916 | tf_op jit(solution)/shard_map/while
  119.5 2.0 copy-start.1
  122.8 8.3 %copy-start = (f32[2,64,64,128]{3,2,1,0:T(8,128)S(1)}, f32[2,64,64,128]{3,2,1,0:T(8,128)}, u32[]{:S(2)}) copy-start(f32[2,64,64,128]{3,2,1,0:T(8,128)} %get-tuple-element.625) | copy-start | bytes 12582916 | tf_op jit(solution)/shard_map/while
  122.8 8.3 %copy-start.5 = (bf16[2,256,64,64]{1,3,2,0:T(8,128)(2,1)S(1)}, bf16[2,256,64,64]{1,3,2,0:T(8,128)(2,1)}, u32[]{:S(2)}) copy-start(bf16[2,256,64,64]{1,3,2,0:T(8,128)(2,1)} %get-tuple-element.638) | copy-start | bytes 12582916 | tf_op jit(solution)/shard_map/while
  131.8 2.0 copy-start.1
  137.9 2.1 copy-start.3
  139.7 88.2 %all-gather.9.cloned.1.call-start = ((), (), s32[]{:S(2)}) async-start(), calls=%async_computation.8 | async-start | bytes 10485760 | tf_op jit(solution)/shard_map/all_gather | solution.py:29
  148.0 52.5 %all-to-all-start.1 = ((bf16[8,1,1024,128]{3,2,1,0:T(8,128)(2,1)}), bf16[8,1,1024,128]{3,2,1,0:T(8,128)(2,1)S(1)}, u32[]{:S(2)}, u32[]{:S(2)}) async-start(bf16[8,1,1024,128]{3,2,1,0:T(8,128)(2,1)} %bitcast.256), calls=%async_computation.2 | async-start | bytes 4194304 | tf_op jit(solution)/shard_map/all_to_all | solution.py:240
  200.5 1.3 copy-start.8
  200.5 6.4 %copy-start.21 = (f32[64]{0:T(128)S(1)}, f32[64]{0:T(128)}, u32[]{:S(2)}) copy-start(f32[64]{0:T(128)} %param.38) | copy-start | bytes 772
  201.8 142.8 %all-to-all-start.2 = ((bf16[8,3,1024,128]{3,2,1,0:T(8,128)(2,1)}), bf16[8,3,1024,128]{3,2,1,0:T(8,128)(2,1)}, u32[]{:S(2)}, u32[]{:S(2)}) async-start(bf16[8,3,1024,128]{3,2,1,0:T(8,128)(2,1)} %bitcast.252), calls=%async_computation.3 | async-start | bytes 12582912 | tf_op jit(solution)/shard_map/all_to_all | solution.py:240
  206.5 45.4 %all-gather.7.cloned.1.call-start = ((), (), s32[]{:S(2)}) async-start(), calls=%async_computation.7 | async-start | bytes 2621440 | tf_op jit(solution)/shard_map/all_gather | solution.py:353
  236.6 15.3 %copy-start.4 = (f32[1,64,64,128]{3,2,1,0:T(8,128)}, f32[1,64,64,128]{3,2,1,0:T(8,128)S(1)}, u32[]{:S(2)}) copy-start(f32[1,64,64,128]{3,2,1,0:T(8,128)S(1)} %get-tuple-element.225) | copy-start | bytes 6291460
  254.4 4.0 %copy-start.2 = (f32[2,1,64,64,128]{4,3,2,1,0:T(8,128)S(1)}, f32[2,1,64,64,128]{4,3,2,1,0:T(8,128)}, u32[]{:S(2)}) copy-start(f32[2,1,64,64,128]{4,3,2,1,0:T(8,128)} %get-tuple-element.705) | copy-start | bytes 12582916 | tf_op jit(solution)/shard_map/while
  258.9 4.0 %copy-start.2 = (f32[2,1,64,64,128]{4,3,2,1,0:T(8,128)S(1)}, f32[2,1,64,64,128]{4,3,2,1,0:T(8,128)}, u32[]{:S(2)}) copy-start(f32[2,1,64,64,128]{4,3,2,1,0:T(8,128)} %get-tuple-element.705) | copy-start | bytes 12582916 | tf_op jit(solution)/shard_map/while
  291.3 14.8 %copy-start.15 = (f32[512]{0:T(512)S(1)}, f32[512]{0:T(512)}, u32[]{:S(2)}) copy-start(f32[512]{0:T(512)} %copy-done.14) | copy-start | bytes 6148
  306.0 8.5 %copy-start.16 = (f32[4096]{0:T(1024)S(1)}, f32[4096]{0:T(1024)}, u32[]{:S(2)}) copy-start(f32[4096]{0:T(1024)} %param.39) | copy-start | bytes 49156
Sparse Core Ops, SparseCore 0:
  17.8 22.1 reduce-scatter.11
  42.6 32.0 reduce-scatter.9
  139.8 28.3 reduce-scatter.7
  169.6 58.2 all-gather.8
  229.3 22.5 all-gather.6

commit v2 on v1

--- a/solution.py
+++ b/solution.py
@@ -6,6 +6,7 @@
 from jax.experimental import pallas as pl
 from jax.experimental.pallas import tpu as pltpu
 from jax.sharding import PartitionSpec as P
+
 
 HEAD_DIM = 64
 STATE_DIM = 128
@@ -100,7 +101,7 @@
     def fold_advance(carried, pieces):
         return (jnp.exp(pieces[1][:, -1])[:, :, None, None] * carried + pieces[0], None)
 
-    final_state, unused = lax.scan(
+    final_state, _ = lax.scan(
         fold_advance, initial, (jnp.moveaxis(block_states, 1, 0), jnp.moveaxis(running_logs, 1, 0))
     )
     return final_state
@@ -286,12 +287,15 @@
         packed = pack_states(flat_states, held_forward(part, used), keep.astype(jnp.int32))
         return packed.reshape((peer_count, high - low) + packed.shape[1:])
 
-    head = exchange(sent(0, 1)).reshape((peer_count,) + flat_states.shape[1:])
+    head_send = sent(0, 1)
+    head = exchange(head_send)
+    head = head.reshape((peer_count,) + flat_states.shape[1:])
     rest = None
     if capacity > 1:
         later_send = sent(1, capacity)
         later_send, head = lax.optimization_barrier((later_send, head))
-        rest = exchange(later_send).reshape((-1,) + flat_states.shape[1:])
+        rest = exchange(later_send)
+        rest = rest.reshape((-1,) + flat_states.shape[1:])
     in_head = from_rank == 0
     first = held_forward(from_peer, in_head)
     later = held_forward(from_peer * max(1, capacity - 1) + from_rank - 1, ~in_head)
@@ -349,8 +353,8 @@
     offsets = jnp.arange(KERNEL - 1, dtype=jnp.int32)
     raw_rows = jnp.concatenate([inputs_inner, inputs_state], axis=2)
     earlier_rows = shifted(raw_rows[:, local_length - KERNEL + 1 :], "seq", 1)
-    initial, head_inner, head_outer = (
-        lax.all_gather(initial_own, "seq", axis=1, tiled=True),
+    initial = lax.all_gather(initial_own, "seq", axis=1, tiled=True)
+    head_inner, head_outer = (
         lax.all_gather(moved_inner[:PREFILLS].astype(jnp.float32), "seq", axis=2, tiled=True),
         lax.all_gather(moved_outer[:PREFILLS].astype(jnp.float32), "seq", axis=2, tiled=True),
     )
@@ -368,6 +372,7 @@
     )
     local_end = fold_states(jnp.zeros_like(block_states[:, 0]), block_states, running_logs)
     device_decay = jnp.exp(jnp.sum(step_sizes * decay_rates, axis=1))
+    device_decay, write_rows = lax.optimization_barrier((device_decay, write_rows))
     every_decay = lax.all_gather(device_decay[None], "seq", axis=0, tiled=True)
     prior_decay, prior_state = entering(
         (device_decay, local_end),
@@ -376,7 +381,7 @@
         (jnp.ones_like(device_decay), jnp.zeros_like(local_end)),
     )
     incoming = prior_state + prior_decay[:, :, None, None] * initial
-    unused_final, inter_parts = run_states(incoming, block_states, running_logs, blocked(read_rows))
+    _, inter_parts = run_states(incoming, block_states, running_logs, blocked(read_rows))
     later_mask = jnp.arange(chain_size)[:, None, None] > chain_index
     suffix = jnp.prod(jnp.where(later_mask, every_decay, 1.0), axis=0)
     whole_decay = jnp.prod(every_decay, axis=0)

time: 364 us -> 361 us (level)
    unnamed x1 -> x0, blocking collectives: 5.64 us -> none
    all_gather x0 -> x1, blocking collectives: none -> 5.27 us  [on_device(): every_decay = lax.all_gather(device_decay[None], 'seq', axis=0, tiled=True)]
    unnamed x54 -> x49, local copies, waits for them, and re-layouts: 15.4 us -> 14.4 us
  transfers between devices with their start and end apart: 9 -> 9, of which waited for: 4 -> 4; matrix products, arithmetic and copies ran while one was open for 44% -> 45% of each run, Pallas kernels for 5% -> 6%
where the time goes in v2:
time: 361 us; the launch traced here: 358 us
  waiting for transfers between devices  87.8 us (24%)
  local copies, waits for them, and re-layouts  82.8 us (23%)
  other arithmetic  61.9 us (17%)
  blocking collectives  37.2 us (10%)
  Pallas kernels  29.7 us (8%)
  matrix products  25.2 us (7%)
  starting transfers between devices  17.6 us (5%)
  between operations  15.3 us (4%)
    all_to_all x3, waiting for transfers between devices, exchange(): lax.all_to_all(source, 'req', split_axis=0, concat_axis=0, tiled=True)  59.8 us
    reshape x2, local copies, waits for them, and re-layouts, assemble(): (intra_part + inter_parts).reshape(value_rows.shape)  31 us
    all_gather x1, blocking collectives, migrate(): every_plan = lax.all_gather(move_plan, 'req')  21 us
    pallas_call x2, Pallas kernels, pack_states(): pl.pallas_call(pack_kernel, grid_spec=pltpu.PrefetchScalarGridSpec(num_sc...  19.7 us
    dot_general x2, matrix products, block_local(): jnp.einsum('hts,shp->thp', weights, value_rows, preferred_element_type=jn...  15.9 us
    all_gather x1, waiting for transfers between devices, on_device(): initial = lax.all_gather(initial_own, 'seq', axis=1, tiled=True)  15.3 us
    all_to_all x3, starting transfers between devices, exchange(): lax.all_to_all(source, 'req', split_axis=0, concat_axis=0, tiled=True)  15 us
    unnamed x49, local copies, waits for them, and re-layouts  14.4 us
  transfers between devices with their start and end apart: 9, of which 4 were waited for; matrix products, arithmetic and copies ran while one was open for 45% of the time, Pallas kernels for 6%

profile of v2, /device:TPU:0, one launch (start us, length us, event | category | flops | bytes accessed | tf_op | source)
XLA Modules:
  0.0 358.1 jit_solution(17458174877999547817)
XLA Ops:
  7.3 2.6 constant_dynamic-update-slice_fusion.1
  10.0 2.1 copy-done.7
  12.1 2.4 collective-permute-start
  15.2 1.6 gather_fusion.2
  20.3 6.6 %all-to-all-start = ((bf16[8,4,3,1088]{3,1,2,0:T(4,128)(2,1)}), bf16[8,4,3,1088]{3,1,2,0:T(4,128)(2,1)S(1)}, u32[]{:S(2)}, u32[]{:S(2)}) async-start(bf16[8,4,3,1088]{3,1,2,0:T(4,128)(2,1)} %copy_select_fusion), calls=%async_computation | async-start | bytes 442368 | tf_op jit(solution)/shard_map/all_to_all | solution.py:241
  27.0 3.7 %copy.136 = f32[1,3,4096]{1,0,2:T(1,128)} copy(f32[1,3,4096]{2,1,0:T(4,128)S(1)} %slice.155) | data formatting | bytes 98304
  30.7 21.0 %all-gather.3 = s32[8,13,2]{1,2,0:T(2,128)S(1)} all-gather(s32[1,13,2]{1,2,0:T(2,128)S(1)} %bitcast.285), channel_id=2, replica_groups=mesh['req'=8,'seq'=4] {'req'}, dimensions={0}, use_global_device_ids=true | all-gather | bytes 936 | tf_op jit(solution)/shard_map/all_gather | solution.py:266
  54.4 5.4 %all_gather.29 = bf16[1,3,256]{1,0,2:T(2,128)(2,1)S(1)} all-gather(bf16[1,3,64]{1,0,2:T(2,128)(2,1)S(1)} %copy.114), channel_id=1, replica_groups=mesh['req'=8,'seq'=4] {'seq'}, dimensions={2}, use_global_device_ids=true | all-gather | bytes 1920 | tf_op jit(solution)/shard_map/all_gather | solution.py:359
  59.9 5.6 %all_gather.28 = bf16[1,3,4096]{2,1,0:T(4,128)(2,1)S(1)} all-gather(bf16[1,3,1024]{2,1,0:T(4,128)(2,1)S(1)} %slice.209), channel_id=1, replica_groups=mesh['req'=8,'seq'=4] {'seq'}, dimensions={2}, use_global_device_ids=true | all-gather | bytes 30720 | tf_op jit(solution)/shard_map/all_gather | solution.py:358
  65.5 3.2 maximum_convert_fusion
  68.7 5.7 %multiply_convert_fusion.5 = bf16[1,512,4352]{2,1,0:T(8,128)(2,1)S(1)} fusion(f32[1,515,4352]{2,1,0:T(8,128)S(1)} %maximum_convert_fusion, f32[4352]{0:T(1024)S(1)} %get-tuple-element.375, f32[4352]{0:T(1024)S(1)} %get-tuple-element.376, f32[4352]{0:T(1024)S(1)} %get-tuple-element.374, f32[4352]{0:T(1024)S(1)} %get-tuple-element.373, f32[4352]{0:T(1024)S(1)} %copy-done.13), kind=kLoop, calls=%fused_computation.75 | loop fusion | flops 28966912 | bytes 40195072 | tf_op jit(solution)/shard_map/convert_element_type | solution.py:51
  74.5 2.9 slice.152
  77.9 12.6 %reshape.684 = bf16[2,256,64,64]{3,2,1,0:T(8,128)(2,1)} reshape(bf16[1,512,4096]{2,1,0:T(8,128)(2,1)} %slice.152) | data formatting | bytes 8388608 | tf_op jit(solution)/shard_map/reshape;reshape | solution.py:78
  90.5 10.5 %copy.117 = bf16[2,256,64,64]{1,3,2,0:T(8,128)(2,1)} copy(bf16[2,256,64,64]{3,2,1,0:T(8,128)(2,1)} %reshape.684) | data formatting | bytes 8388608 | tf_op jit(solution)/shard_map/while | solution.py:86
  101.0 24.7 %while.53 = (s32[]{:T(128)}, f32[2,256,64,64]{1,3,2,0:T(8,128)}, f32[2,64,64,128]{3,2,1,0:T(8,128)}, f32[2,256,64]{1,2,0:T(8,128)S(1)}, bf16[2,256,64,64]{1,3,2,...) while((s32[]{:T(128)}, f32[2,256,64,64]{1,3,2,0:T(8,128)}, ...), condition=%wide.region_12.13_spmd, body=%wide.region_9.12_spmd.sunk | while | flops 852639936 | bytes 62990296 | solution.py:86
  102.3 7.9 %bitcast_dynamic-update-slice_fusion.8 = f32[2,256,64,64]{1,3,2,0:T(8,128)} fusion(f32[2,256,64,64]{1,3,2,0:T(8,128)} %get-tuple-element.626, s32[]{:T(128)S(6)} %copy.183, f32[64,256]{1,0:T(8,128)S(1)} %bitcast.268, f32[64,256]{1,0:T(8,128)S(1)} %get-tuple-element.594, f32[256,256]{1,0:T(8,128)S(1)} %fusion.87, ...), kind=kOutput, calls=%fused_computation.22.clone.1 | convolution fusion | flops 562036736 | bytes 6816768 | tf_op jit(solution)/shard_map/while/body/eval_jaxpr/hts,shp->thp/dot_general | solution.py:66
  111.4 1.9 copy-done.1
  114.6 7.9 %bitcast_dynamic-update-slice_fusion.8 = f32[2,256,64,64]{1,3,2,0:T(8,128)} fusion(f32[2,256,64,64]{1,3,2,0:T(8,128)} %get-tuple-element.626, s32[]{:T(128)S(6)} %copy.183, f32[64,256]{1,0:T(8,128)S(1)} %bitcast.268, f32[64,256]{1,0:T(8,128)S(1)} %get-tuple-element.594, f32[256,256]{1,0:T(8,128)S(1)} %fusion.87, ...), kind=kOutput, calls=%fused_computation.22.clone.1 | convolution fusion | flops 562036736 | bytes 6816768 | tf_op jit(solution)/shard_map/while/body/eval_jaxpr/hts,shp->thp/dot_general | solution.py:66
  123.7 1.9 copy-done.1
  125.8 3.9 %while.55 = (s32[]{:T(128)}, f32[1,64,64,128]{3,2,1,0:T(8,128)S(1)}, f32[2,1,256,64]{3,2,1,0:T(8,128)S(1)}, f32[2,1,64,64,128]{4,3,2,1,0:T(8,128)}, s32[]{:T(128)}, /*index=5*/s32[]{:T(128)}) while((s32[]{:T(128)}, f32[1,64,64,128]{3,2,1,0:T(8,128)S(1)}, f32[2,1,256,64]{3,2,1,0:T(8,128)S(1)}, f32[2,1,64,64,128]{4,3,2,1,0:T(8,128)}, ...), condition=%wide.region_14.15_spmd.clone, body=%wide.region_13.14_spmd.clone.sunk | while | flops 1572867 | bytes 6423391 | solution.py:104
  125.8 1.9 bitcast_add_fusion.8
  127.8 1.9 bitcast_add_fusion.8
  129.7 5.3 %all-gather.4 = f32[4,1,64]{2,1,0:T(1,128)S(1)} all-gather(f32[1,1,64]{2,1,0:T(1,128)S(1)} %bitcast.286), channel_id=3, replica_groups=mesh['req'=8,'seq'=4] {'seq'}, dimensions={0}, use_global_device_ids=true | all-gather | bytes 1280 | tf_op jit(solution)/shard_map/all_gather | solution.py:376
  135.1 1.6 broadcast_multiply_fusion
  138.9 6.0 %shard_map.184 = bf16[8,1024,128]{2,1,0:T(8,128)(2,1)} custom-call(s32[8]{0:T(128)} %select_reduce_fusion.10.source_ref, s32[8]{0:T(128)} %select_reduce_fusion.9.keep_ref, f32[13,1024,128]{2,1,0:T(8,128)} %bitcast.252), custom_call_target="tpu_custom_call" | custom-call | flops 1048576 | bytes 6291456 | tf_op jit(solution)/shard_map/pallas_call | solution.py:168
  144.9 3.6 %all-to-all-start.1 = ((bf16[8,1,1024,128]{3,2,1,0:T(8,128)(2,1)}), bf16[8,1,1024,128]{3,2,1,0:T(8,128)(2,1)S(1)}, u32[]{:S(2)}, u32[]{:S(2)}) async-start(bf16[8,1,1024,128]{3,2,1,0:T(8,128)(2,1)} %bitcast.258), calls=%async_computation.2 | async-start | bytes 4194304 | tf_op jit(solution)/shard_map/all_to_all | solution.py:241
  150.3 13.7 %shard_map.183 = bf16[24,1024,128]{2,1,0:T(8,128)(2,1)} custom-call(s32[24]{0:T(128)} %select_reduce_fusion.2.source_ref, s32[24]{0:T(128)} %select_reduce_fusion.4.keep_ref, f32[13,1024,128]{2,1,0:T(8,128)} %bitcast.253), custom_call_target="tpu_custom_call" | custom-call | flops 3145728 | bytes 18874368 | tf_op jit(solution)/shard_map/pallas_call | solution.py:168
  164.0 33.4 %all-to-all-done.1 = bf16[8,1,1024,128]{3,2,1,0:T(8,128)(2,1)S(1)} async-done(((bf16[8,1,1024,128]{3,2,1,0:T(8,128)(2,1)}), bf16[8,1,1024,128]{3,2,1,0:T(8,128)(2,1)S(1)}, u32[]{:S(2)}, u32[]{:S(2)}) %all-to-all-start.1) | async-done | bytes 2097184 | tf_op jit(solution)/shard_map/all_to_all | solution.py:241
  198.8 4.8 %all-to-all-start.2 = ((bf16[8,3,1024,128]{3,2,1,0:T(8,128)(2,1)}), bf16[8,3,1024,128]{3,2,1,0:T(8,128)(2,1)}, u32[]{:S(2)}, u32[]{:S(2)}) async-start(bf16[8,3,1024,128]{3,2,1,0:T(8,128)(2,1)} %bitcast.254), calls=%async_computation.3 | async-start | bytes 12582912 | tf_op jit(solution)/shard_map/all_to_all | solution.py:241
  211.1 2.0 fusion.46
  213.0 12.1 %all-gather.10.cloned.1.call-done = f32[4,64,64,128]{3,2,1,0:T(8,128)} async-done(((f32[1,64,64,128]{3,2,1,0:T(8,128)}), f32[4,64,64,128]{3,2,1,0:T(8,128)}) %all-gather.10.cloned.1.call-update) | async-done | bytes 8388624 | tf_op jit(solution)/shard_map/all_gather | solution.py:30
  225.2 8.7 %while.56 = (s32[]{:T(128)}, f32[1,64]{1,0:T(1,128)S(1)}, f32[1,64,64,128]{3,2,1,0:T(8,128)S(1)}, s32[]{:T(128)}, f32[4,1,64]{2,1,0:T(1,128)S(1)}, /*index=5*/f32[4,1,64,64,128]{4,3,2,1,0:T(8,128)}, s32[]{:T(128)}, s32[]{:T(128)}) while((s32[]{:T(128)}, f32[1,64]{1,0:T(1,128)S(1)}, f32[1,64,64,128]{3,2,1,0:T(8,128)S(1)}, ...), condition=%wide.region_29.30_spmd.clone, body=%wide.region_28.29_spmd.clone.sunk | while | flops 2097348 | bytes 6293119 | solution.py:42
  225.2 2.1 fusion.93
  227.3 2.1 fusion.93
  229.5 2.1 fusion.93
  231.6 2.2 fusion.93
  233.8 15.3 %all-gather.8.cloned.1.call-done = f32[1,64,64,128]{3,2,0,1:T(8,128)} async-done(((f32[1,16,64,128]{3,2,0,1:T(8,128)}), f32[1,64,64,128]{3,2,0,1:T(8,128)}) %all-gather.8.cloned.1.call-update) | async-done | bytes 2097168 | tf_op jit(solution)/shard_map/all_gather | solution.py:356
  249.2 2.5 fusion.45
  251.7 8.9 %while.54 = (s32[]{:T(128)}, f32[1,64,64,128]{3,2,1,0:T(8,128)S(1)}, f32[2,1,256,64,64]{2,4,3,1,0:T(8,128)}, f32[2,1,256,64]{2,3,1,0:T(8,128)S(1)}, f32[2,1,64,6...) while((s32[]{:T(128)}, f32[1,64,64,128]{3,2,1,0:T(8,128)S(1)}, ...), condition=%wide.region_31.32_spmd, body=%wide.region_30.31_spmd.sunk | while | flops 1612709888 | bytes 29689720 | solution.py:126
  251.7 3.7 %bitcast_dynamic-update-slice_fusion.11 = f32[2,1,256,64,64]{2,4,3,1,0:T(8,128)} fusion(f32[2,1,256,64,64]{2,4,3,1,0:T(8,128)} %get-tuple-element.698, s32[]{:T(128)S(6)} %copy.209, f32[1,64,64,128]{3,2,1,0:T(8,128)S(1)} %get-tuple-element.697, f32[256,64]{0,1:T(8,128)S(1)} %get-tuple-element.603, bf16[2,1,256,128]{3,2,1,0:T(8,128)(2,1)S(1)} %get-tuple-element.708), kind=kOutput, calls=%fused_computation.55.clone.1 | convolution fusion | flops 1611661312 | bytes 6423552 | tf_op jit(solution)/shard_map/while/body/eval_jaxpr/bqn,bhpn->bqhp/dot_general | solution.py:115
  256.2 3.8 %bitcast_dynamic-update-slice_fusion.11 = f32[2,1,256,64,64]{2,4,3,1,0:T(8,128)} fusion(f32[2,1,256,64,64]{2,4,3,1,0:T(8,128)} %get-tuple-element.698, s32[]{:T(128)S(6)} %copy.209, f32[1,64,64,128]{3,2,1,0:T(8,128)S(1)} %get-tuple-element.697, f32[256,64]{0,1:T(8,128)S(1)} %get-tuple-element.603, bf16[2,1,256,128]{3,2,1,0:T(8,128)(2,1)S(1)} %get-tuple-element.708), kind=kOutput, calls=%fused_computation.55.clone.1 | convolution fusion | flops 1611661312 | bytes 6423552 | tf_op jit(solution)/shard_map/while/body/eval_jaxpr/bqn,bhpn->bqhp/dot_general | solution.py:115
  260.6 11.7 %bitcast_add_fusion.3 = f32[2,256,64,64]{1,3,2,0:T(8,128)} fusion(f32[2,256,64,64]{1,3,2,0:T(8,128)} %get-tuple-element.226, f32[2,1,256,64,64]{2,4,3,1,0:T(8,128)} %get-tuple-element.229), kind=kLoop, calls=%fused_computation.80 | loop fusion | flops 2097152 | bytes 25165824 | tf_op jit(solution)/shard_map/add | solution.py:139
  272.3 16.3 %copy.135 = f32[2,256,64,64]{3,2,1,0:T(8,128)} copy(f32[2,256,64,64]{1,3,2,0:T(8,128)} %bitcast_add_fusion.3) | data formatting | bytes 16777216 | tf_op jit(solution)/shard_map/reshape | solution.py:139
  288.5 14.8 %reshape.685 = f32[1,512,4096]{2,1,0:T(8,128)} reshape(f32[2,256,64,64]{3,2,1,0:T(8,128)} %copy.135) | data formatting | bytes 16777216 | tf_op jit(solution)/shard_map/reshape | solution.py:139
  303.3 8.5 %multiply_reduce_fusion = (f32[512]{0:T(512)S(1)}, f32[1,512,4096]{2,1,0:T(8,128)S(1)}) fusion(bf16[1,512,4096]{2,1,0:T(8,128)(2,1)} %param.31, f32[512]{0:T(512)S(1)} %copy-done.15, f32[1,512,4096]{2,1,0:T(8,128)} %reshape.685, bf16[1,512,4352]{2,1,0:T(8,128)(2,1)} %copy-done.6, f32[4096]{0:T(1024)S(1)} %mul.342), kind=kLoop, calls=%fused_computation.82 | loop fusion | flops 29359616 | bytes 25186304 | tf_op jit(solution)/shard_map/reduce_sum | solution.py:148
  311.8 3.5 multiply_convert_fusion.6
  315.2 26.3 %all-to-all-done.2 = bf16[8,3,1024,128]{3,2,1,0:T(8,128)(2,1)} async-done(((bf16[8,3,1024,128]{3,2,1,0:T(8,128)(2,1)}), bf16[8,3,1024,128]{3,2,1,0:T(8,128)(2,1)}, u32[]{:S(2)}, u32[]{:S(2)}) %all-to-all-start.2) | async-done | bytes 6291488 | tf_op jit(solution)/shard_map/all_to_all | solution.py:241
  341.6 10.0 %shard_map.185 = f32[13,1024,128]{2,1,0:T(8,128)} custom-call(s32[13]{0:T(128)} %select_reduce_fusion.7.first_ref, s32[13]{0:T(128)} %select_reduce_fusion.5.later_ref, s32[13]{0:T(128)} %copy-done.18, f32[1,1024,128]{2,1,0:T(8,128)} %bitcast.267, bf16[8,1024,128]{2,1,0:T(8,128)(2,1)} %bitcast.257, bf16[24,1024,128]{2,1,0:T(8,128)(2,1)} %bitcast.53.refs_2_), custom_call_target="tpu_custom_call" | custom-call | flops 1703936 | bytes 10223616 | tf_op jit(solution)/shard_map/pallas_call | solution.py:215
  (215 shorter events, 25.8 us)
Async XLA Ops:
  7.2 2.7 copy-start.9
  7.2 10.5 %copy-start.19 = (s32[13,2]{0,1:T(2,128)S(1)}, s32[13,2]{0,1:T(2,128)}, u32[]{:S(2)}) copy-start(s32[13,2]{0,1:T(2,128)} %param.27) | copy-start | bytes 316
  7.2 10.5 %copy-start.17 = (bf16[13,3,64]{2,0,1:T(8,128)(2,1)S(1)}, bf16[13,3,64]{2,0,1:T(8,128)(2,1)}, u32[]{:S(2)}) copy-start(bf16[13,3,64]{2,0,1:T(8,128)(2,1)} %param.26) | copy-start | bytes 14980
  7.2 10.5 %copy-start.10 = (bf16[13,3,1024]{2,0,1:T(8,128)(2,1)S(1)}, bf16[13,3,1024]{2,0,1:T(8,128)(2,1)}, u32[]{:S(2)}) copy-start(bf16[13,3,1024]{2,0,1:T(8,128)(2,1)} %param.25) | copy-start | bytes 239620
  7.2 10.6 %copy-start.23 = (s32[13]{0:T(128)S(1)}, s32[13]{0:T(128)}, u32[]{:S(2)}) copy-start(s32[13]{0:T(128)} %param.28) | copy-start | bytes 160
  7.2 198.3 %reduce-scatter.12.cloned.1.call-start = ((), (), s32[]{:S(2)}) async-start(), calls=%async_computation.10 | async-start | bytes 163840
  9.9 42.8 %copy-start.22 = (f32[64]{0:T(128)S(1)}, f32[64]{0:T(128)}, u32[]{:S(2)}) copy-start(f32[64]{0:T(128)} %param.37) | copy-start | bytes 772
  9.9 42.8 %copy-start.12 = (bf16[1,512,64]{1,2,0:T(8,128)(2,1)S(1)}, bf16[1,512,64]{1,2,0:T(8,128)(2,1)}, u32[]{:S(2)}) copy-start(bf16[1,512,64]{1,2,0:T(8,128)(2,1)} %param.32) | copy-start | bytes 196612
  9.9 42.8 %copy-start.20 = (f32[64]{0:T(128)S(1)}, f32[64]{0:T(128)}, u32[]{:S(2)}) copy-start(f32[64]{0:T(128)} %param.36) | copy-start | bytes 772
  9.9 43.2 %copy-start.11 = (f32[4,4352]{1,0:T(4,128)S(1)}, f32[4,4352]{1,0:T(4,128)}, u32[]{:S(2)}) copy-start(f32[4,4352]{1,0:T(4,128)} %param.34) | copy-start | bytes 208900
  9.9 2.1 copy-start.7
  12.1 53.4 %collective-permute-start = (bf16[1,3,4352]{2,1,0:T(4,128)(2,1)S(1)}, bf16[1,3,4352]{2,1,0:T(4,128)(2,1)S(1)}, u32[]{:S(2)}, u32[]{:S(2)}) collective-permute-start(bf16[1,3,4352]{2,1,0:T(4,128)(2,1)S(1)} %slice.147), channel_id=1, source_target_pairs={{0,1},{1,2},{2,3},{4,5},{5,6},{6,7},{8,9},{9,10},{10,11},{12,13},{... | collective-permute-start | bytes 78344 | tf_op jit(solution)/shard_map/ppermute | solution.py:25
  20.3 33.0 %all-to-all-start = ((bf16[8,4,3,1088]{3,1,2,0:T(4,128)(2,1)}), bf16[8,4,3,1088]{3,1,2,0:T(4,128)(2,1)S(1)}, u32[]{:S(2)}, u32[]{:S(2)}) async-start(bf16[8,4,3,1088]{3,1,2,0:T(4,128)(2,1)} %copy_select_fusion), calls=%async_computation | async-start | bytes 442368 | tf_op jit(solution)/shard_map/all_to_all | solution.py:241
  26.9 179.5 %reduce-scatter.10.cloned.1.call-start = ((), (), s32[]{:S(2)}) async-start(), calls=%async_computation.9 | async-start | bytes 2621440
  30.7 180.4 %reduce-scatter.8.cloned.1.call-start = ((), (), s32[]{:S(2)}) async-start(), calls=%async_computation.6 | async-start | bytes 2621440 | tf_op jit(solution)/shard_map/reduce_scatter | solution.py:395
  52.6 152.2 %copy-start.18 = (s32[13]{0:T(128)}, s32[13]{0:T(128)S(1)}, u32[]{:S(2)}) copy-start(s32[13]{0:T(128)S(1)} %get-tuple-element.377.pick_ref) | copy-start | bytes 160
  52.7 1.4 copy-start.14
  65.5 3.2 copy-start.13
  74.5 3.4 copy-start.6
  102.3 8.3 %copy-start = (f32[2,64,64,128]{3,2,1,0:T(8,128)S(1)}, f32[2,64,64,128]{3,2,1,0:T(8,128)}, u32[]{:S(2)}) copy-start(f32[2,64,64,128]{3,2,1,0:T(8,128)} %get-tuple-element.627) | copy-start | bytes 12582916 | tf_op jit(solution)/shard_map/while
  102.3 8.3 %copy-start.5 = (bf16[2,256,64,64]{1,3,2,0:T(8,128)(2,1)S(1)}, bf16[2,256,64,64]{1,3,2,0:T(8,128)(2,1)}, u32[]{:S(2)}) copy-start(bf16[2,256,64,64]{1,3,2,0:T(8,128)(2,1)} %get-tuple-element.640) | copy-start | bytes 12582916 | tf_op jit(solution)/shard_map/while
  111.3 2.0 copy-start.1
  114.6 8.3 %copy-start = (f32[2,64,64,128]{3,2,1,0:T(8,128)S(1)}, f32[2,64,64,128]{3,2,1,0:T(8,128)}, u32[]{:S(2)}) copy-start(f32[2,64,64,128]{3,2,1,0:T(8,128)} %get-tuple-element.627) | copy-start | bytes 12582916 | tf_op jit(solution)/shard_map/while
  114.6 8.3 %copy-start.5 = (bf16[2,256,64,64]{1,3,2,0:T(8,128)(2,1)S(1)}, bf16[2,256,64,64]{1,3,2,0:T(8,128)(2,1)}, u32[]{:S(2)}) copy-start(bf16[2,256,64,64]{1,3,2,0:T(8,128)(2,1)} %get-tuple-element.640) | copy-start | bytes 12582916 | tf_op jit(solution)/shard_map/while
  123.6 2.0 copy-start.1
  129.7 7.0 %copy-start.3 = (f32[1,64,64,128]{3,2,1,0:T(8,128)}, f32[1,64,64,128]{3,2,1,0:T(8,128)S(1)}, u32[]{:S(2)}) copy-start(f32[1,64,64,128]{3,2,1,0:T(8,128)S(1)} %get-tuple-element.222) | copy-start | bytes 6291460
  136.7 88.5 %all-gather.10.cloned.1.call-start = ((), (), s32[]{:S(2)}) async-start(), calls=%async_computation.8 | async-start | bytes 10485760 | tf_op jit(solution)/shard_map/all_gather | solution.py:30
  144.9 52.6 %all-to-all-start.1 = ((bf16[8,1,1024,128]{3,2,1,0:T(8,128)(2,1)}), bf16[8,1,1024,128]{3,2,1,0:T(8,128)(2,1)S(1)}, u32[]{:S(2)}, u32[]{:S(2)}) async-start(bf16[8,1,1024,128]{3,2,1,0:T(8,128)(2,1)} %bitcast.258), calls=%async_computation.2 | async-start | bytes 4194304 | tf_op jit(solution)/shard_map/all_to_all | solution.py:241
  197.5 1.3 copy-start.8
  197.5 6.2 %copy-start.21 = (f32[64]{0:T(128)S(1)}, f32[64]{0:T(128)}, u32[]{:S(2)}) copy-start(f32[64]{0:T(128)} %param.38) | copy-start | bytes 772
  198.8 142.8 %all-to-all-start.2 = ((bf16[8,3,1024,128]{3,2,1,0:T(8,128)(2,1)}), bf16[8,3,1024,128]{3,2,1,0:T(8,128)(2,1)}, u32[]{:S(2)}, u32[]{:S(2)}) async-start(bf16[8,3,1024,128]{3,2,1,0:T(8,128)(2,1)} %bitcast.254), calls=%async_computation.3 | async-start | bytes 12582912 | tf_op jit(solution)/shard_map/all_to_all | solution.py:241
  203.5 45.6 %all-gather.8.cloned.1.call-start = ((), (), s32[]{:S(2)}) async-start(), calls=%async_computation.7 | async-start | bytes 2621440 | tf_op jit(solution)/shard_map/all_gather | solution.py:356
  233.8 15.3 %copy-start.4 = (f32[1,64,64,128]{3,2,1,0:T(8,128)}, f32[1,64,64,128]{3,2,1,0:T(8,128)S(1)}, u32[]{:S(2)}) copy-start(f32[1,64,64,128]{3,2,1,0:T(8,128)S(1)} %get-tuple-element.227) | copy-start | bytes 6291460
  251.7 4.0 %copy-start.2 = (f32[2,1,64,64,128]{4,3,2,1,0:T(8,128)S(1)}, f32[2,1,64,64,128]{4,3,2,1,0:T(8,128)}, u32[]{:S(2)}) copy-start(f32[2,1,64,64,128]{4,3,2,1,0:T(8,128)} %get-tuple-element.707) | copy-start | bytes 12582916 | tf_op jit(solution)/shard_map/while
  256.1 4.0 %copy-start.2 = (f32[2,1,64,64,128]{4,3,2,1,0:T(8,128)S(1)}, f32[2,1,64,64,128]{4,3,2,1,0:T(8,128)}, u32[]{:S(2)}) copy-start(f32[2,1,64,64,128]{4,3,2,1,0:T(8,128)} %get-tuple-element.707) | copy-start | bytes 12582916 | tf_op jit(solution)/shard_map/while
  288.5 14.8 %copy-start.15 = (f32[512]{0:T(512)S(1)}, f32[512]{0:T(512)}, u32[]{:S(2)}) copy-start(f32[512]{0:T(512)} %copy-done.14) | copy-start | bytes 6148
  303.3 8.5 %copy-start.16 = (f32[4096]{0:T(1024)S(1)}, f32[4096]{0:T(1024)}, u32[]{:S(2)}) copy-start(f32[4096]{0:T(1024)} %param.39) | copy-start | bytes 49156
Sparse Core Ops, SparseCore 0:
  17.8 22.2 reduce-scatter.11
  42.6 31.3 reduce-scatter.9
  136.8 28.6 reduce-scatter.7
  166.9 58.2 all-gather.9
  226.6 22.5 all-gather.7
